TPU v7x, 32 devices: a whole 2x2x4 slice. The times are simulated.
32 devices in a mesh: gx: 4 (over z), gy: 8 (over y, x, core).
Axes of the slice: x: 2, y: 2, z: 4, core: 2. Of those that a mesh axis runs over, the one named last changes fastest.
Arguments:
- rhs: float32 [4, 128, 16384], P(None, None, ('gx', 'gy')), may hold values from -6 to 6
- offsets: float32 [3, 128, 16384], P(None, None, ('gx', 'gy')), may hold values from -4 to 4
- lengths: float32 [16384], P(('gx', 'gy')), may hold values from 1 to 4
- bucket: int32 [16384, 1], P(('gx', 'gy')), may hold values from 0 to 3; in each aligned block of 512 rows (0 to 511, 512 to 1023, ...) at most 128 rows name the same one
- attach: int32 [16384], P(('gx', 'gy')), may hold values from 0 to 511
- operator: float32 [4, 512, 512], P('gx'), may hold values from -0.25 to 0.25
- inverse: float32 [4, 512, 512], P('gx'), as said below
- mobility: float32 [36, 2048], P(None, ('gx', 'gy')), may hold values from -2.5 to 2.5
Outputs:
- velocity: float32 [4, 128, 16384], P(None, None, ('gx', 'gy'))
Inputs may be any that keep to these rules, and one draw needn't show every extreme that they name: Bucket b owns fibers of 16 * 2^(b mod 4) nodes. Among the 512 fibers of one device no bucket has more than 128, and in every draw some bucket has exactly 128 there. `inverse`: identity plus a dense full-rank part.
All inputs are finite; a program needn't handle non-finite values.
Results may differ from a plain program's by a relative error of at most 0.0003.
Values sent between devices are 32-bit elements; how exact they have to be, the bound alone decides.
No kernel may reach another device: no remote copies, remote signals or barrier semaphores. Data moves between devices by JAX's collectives and lax.ppermute only.
A program may use at most 64 MiB of HBM per device.

v0:
```python
import jax
import jax.numpy as jnp
from jax import lax
from jax.experimental import pallas as pl
from jax.experimental.pallas import tpu as pltpu
from jax.sharding import PartitionSpec as P


NODE_MIN = 16
LEVELS = 4
ITERS = 4
SLOT_CAP = 128
VMEM_LIMIT = 32 << 20
F32 = jnp.float32
BF16 = jnp.bfloat16
NN = (((1,), (0,)), ((), ()))
NT = (((1,), (1,)), ((), ()))


def split(value):
    high = value.astype(BF16)
    low = (value - high.astype(F32)).astype(BF16)
    return high, low


def mm(a, b, dims=NN):
    return lax.dot_general(a, b, dims, preferred_element_type=F32)


def pick(value, onehot, dims):
    high, low = split(value)
    return mm(high, onehot, dims) + mm(low, onehot, dims)


VM = pl.BlockSpec(memory_space=pltpu.VMEM)
ANY = pl.BlockSpec(memory_space=pl.ANY)


def near(*values):
    return tuple(pltpu.with_memory_space_constraint(v, pltpu.VMEM) for v in values)


def call(kernel, outs, far=(), values=(), scratch=(), far_out=False, flops=0):
    if far_out:
        out_shape = tuple(jax.ShapeDtypeStruct(shape, kind) for shape, kind in outs)
    else:
        out_shape = tuple(pltpu.VMEM(shape, kind) for shape, kind in outs)
    return pl.pallas_call(
        kernel,
        out_shape=out_shape,
        in_specs=[ANY] * len(far) + [VM] * len(values),
        out_specs=tuple(ANY if far_out else VM for _ in outs),
        scratch_shapes=list(scratch),
        compiler_params=pltpu.CompilerParams(vmem_limit_bytes=VMEM_LIMIT),
        cost_estimate=pl.CostEstimate(flops=flops, transcendentals=0, bytes_accessed=1 << 20),
    )(*far, *near(*values))


def take_share(operator, inverse, rows):
    width = operator.shape[1]

    def kernel(op_ref, inv_ref, a_ref, sem):
        seat = lax.axis_index("gy")

        def load(src):
            copy = pltpu.make_async_copy(src.at[pl.ds((seat // 2) * rows, rows)], a_ref, sem)
            copy.start()
            copy.wait()

        @pl.when(seat % 2 == 0)
        def _():
            load(inv_ref)

        @pl.when(seat % 2 != 0)
        def _():
            load(op_ref)

    return call(
        kernel,
        [((rows, width), F32)],
        far=(operator, inverse),
        scratch=[pltpu.SemaphoreType.DMA],
        flops=1 << 20,
    )[0]


def pack_blocks(operator, inverse, mobility, nodes):
    half, quarter = nodes // 2, nodes // 4
    entries, seat_lanes = mobility.shape
    groups = -(-entries // 8)
    assert 2 * seat_lanes == nodes and groups <= 8

    def kernel(op_ref, inv_ref, mob_ref, mid_ref, small_ref, ext_ref, buf, sems):
        seat = lax.axis_index("gy")
        level = lax.axis_index("gx") % LEVELS

        def load(src):
            copies = [
                pltpu.make_async_copy(
                    src.at[pl.ds(c * nodes, half)], buf.at[pl.ds(c * half, half)], sems.at[c]
                )
                for c in range(4)
            ]
            for copy in copies:
                copy.start()
            for copy in copies:
                copy.wait()

        @pl.when(seat % 2 == 0)
        def _():
            load(inv_ref)

        @pl.when(seat % 2 != 0)
        def _():
            load(op_ref)

        lane = lax.broadcasted_iota(jnp.int32, (4 * half, nodes), 1)
        for pair in range(2):
            first = buf[:, pl.ds(2 * pair * nodes, nodes)]
            second = pltpu.roll(buf[:, pl.ds((2 * pair + 1) * nodes, nodes)], half, 1)
            mid_ref[:, pl.ds(pair * nodes, nodes)] = jnp.where(lane < half, first, second)
        count = jnp.left_shift(jnp.int32(NODE_MIN), level)
        lane = lax.broadcasted_iota(jnp.int32, (quarter, nodes), 1)
        row = lax.broadcasted_iota(jnp.int32, (quarter, nodes), 0)
        keep = ((lane % quarter) < count) & (row < count)
        for c in range(4):
            block = jnp.zeros((quarter, nodes), F32)
            for d in range(4):
                part = buf[pl.ds(c * half, quarter), pl.ds(d * nodes, nodes)]
                if d:
                    part = pltpu.roll(part, d * quarter, 1)
                block = jnp.where(lane // quarter == d, part, block)
            small_ref[pl.ds(c * quarter, quarter), :] = jnp.where(keep, block, 0.0)
        parts = []
        for g in range(8):
            size = max(0, min(8, entries - 8 * g))
            part = jnp.zeros((8, seat_lanes), F32)
            if size:
                part = mob_ref[pl.ds(8 * g, size), :]
                if size < 8:
                    part = jnp.concatenate([part, jnp.zeros((8 - size, seat_lanes), F32)], axis=0)
            parts.append(part)
        ext_ref[...] = jnp.concatenate(parts, axis=1)

    return call(
        kernel,
        [
            ((4 * half, 4 * half), F32),
            ((4 * quarter, 4 * quarter), F32),
            ((8, 8 * seat_lanes), F32),
        ],
        far=(operator, inverse),
        values=(mobility,),
        scratch=[pltpu.VMEM((4 * half, 4 * nodes), F32), pltpu.SemaphoreType.DMA((4,))],
        flops=1 << 20,
    )


def grade(buckets):
    small = [b for b in range(buckets) if b % LEVELS < LEVELS - 2]
    mid = [b for b in range(buckets) if b % LEVELS == LEVELS - 2]
    top = [b for b in range(buckets) if b % LEVELS == LEVELS - 1]
    return small, mid, top


def sort_fibers(bucket, attach, lengths, rhs, offsets, buckets, centres, nodes):
    fibers = bucket.shape[1]
    groups = grade(buckets)
    order = [b for group in groups for b in group]
    spans = [nodes // 4, nodes // 2, nodes]

    def kernel(bk_ref, at_ref, len_ref, rhs_ref, off_ref, oh_ref, s_ref, *rest):
        sorted_refs, aux_ref = rest[:3], rest[3]
        bk = bk_ref[...]
        ids = lax.broadcasted_iota(jnp.int32, (max(8, buckets), fibers), 0)
        mark = (ids == bk).astype(BF16)
        upper = (
            lax.broadcasted_iota(jnp.int32, (fibers, fibers), 0)
            < lax.broadcasted_iota(jnp.int32, (fibers, fibers), 1)
        ).astype(BF16)
        before = mm(mark, upper)
        place = jnp.sum(jnp.where(ids == bk, before, 0.0), axis=0, keepdims=True).astype(jnp.int32)
        slot = lax.broadcasted_iota(jnp.int32, (SLOT_CAP, fibers), 0)
        for k, b in enumerate(order):
            hot = (slot == place) & (bk == b)
            oh_ref[pl.ds(k * SLOT_CAP, SLOT_CAP), :] = hot.astype(BF16)
        onehot = oh_ref[...]
        centre = (
            lax.broadcasted_iota(jnp.int32, (centres, fibers), 0) == at_ref[...]
        ).astype(BF16)
        s_ref[...] = mm(onehot, centre, NT).astype(BF16)
        length = len_ref[...]
        row = lax.broadcasted_iota(jnp.int32, (8, fibers), 0)
        aux = jnp.where(row == 0, 0.3 / length, jnp.where(row == 1, length, 0.0))
        aux_ref[...] = pick(aux, onehot, NT)
        start = 0
        for group, span, ref in zip(groups, spans, sorted_refs):
            hot = oh_ref[pl.ds(start, len(group) * SLOT_CAP), :]
            start += len(group) * SLOT_CAP
            for c in range(7):
                src = rhs_ref[c, pl.ds(0, span), :] if c < 4 else off_ref[c - 4, pl.ds(0, span), :]
                ref[pl.ds(c * span, span), :] = pick(src, hot, NT)

    return call(
        kernel,
        [
            ((buckets * SLOT_CAP, fibers), BF16),
            ((buckets * SLOT_CAP, centres), BF16),
            *[
                ((7 * span, len(group) * SLOT_CAP), F32)
                for group, span in zip(groups, spans)
            ],
            ((8, buckets * SLOT_CAP), F32),
        ],
        values=(bucket, attach, lengths, rhs, offsets),
        flops=1 << 30,
    )


def product(matrix, vector):
    high, low = matrix
    v_high, v_low = split(vector)
    width = vector.shape[1]
    both = mm(high, jnp.concatenate([v_high, v_low], axis=1))
    return both[:, :width] + both[:, width:] + mm(low, v_high)


def couple(geometry, vector, n):
    u = [vector[c * n:(c + 1) * n] for c in range(4)]
    o = [geometry[c * n:(c + 1) * n] for c in range(3)]
    along = o[0] * u[0] + o[1] * u[1] + o[2] * u[2]
    pull = along + u[3]
    return 0.15 * jnp.concatenate([o[0] * pull, o[1] * pull, o[2] * pull, along], axis=0)


def sweeps(systems):
    vectors = [product(inverse, source) for inverse, _, source, _, _, _ in systems]
    for _ in range(ITERS):
        forces = [
            source - factor * product(stiffness, v) - couple(geometry, v, n)
            for v, (_, stiffness, source, geometry, factor, n) in zip(vectors, systems)
        ]
        vectors = [product(system[0], force) for force, system in zip(forces, systems)]
    return vectors


def wrench_rows(vector, geometry, length, n, count):
    u = [vector[c * n:(c + 1) * n] for c in range(3)]
    o = [geometry[c * n:(c + 1) * n] for c in range(3)]
    sums = [jnp.sum(v, axis=0, keepdims=True) for v in u]
    for a, b in ((1, 2), (2, 0), (0, 1)):
        sums.append(jnp.sum(o[a] * u[b] - o[b] * u[a], axis=0, keepdims=True))
    zero = jnp.zeros_like(sums[0])
    return (length / count) * jnp.concatenate(sums + [zero, zero], axis=0)


def solve_low(smalls, mids, sorted_small, sorted_mid, aux, slots, buckets, nodes):
    small, mid, _ = grade(buckets)
    centres = slots.shape[1]
    half, quarter = nodes // 2, nodes // 4

    def kernel(so_ref, st_ref, mo_ref, mt_ref, ss_ref, sm_ref, aux_ref, slot_ref, xs_ref, xm_ref, t_ref):
        gx = lax.axis_index("gx")
        first = lax.axis_index("gy") % 2 == 0
        systems, lengths, counts = [], [], []
        for k, b in enumerate(small + mid):
            lanes = pl.ds(k * SLOT_CAP, SLOT_CAP)
            if k < len(small):
                index = lax.rem(b - gx + buckets, buckets)
                mine, theirs, ref, here, n = so_ref[index], st_ref[index], ss_ref, lanes, quarter
            else:
                j = k - len(small)
                here = pl.ds(j * SLOT_CAP, SLOT_CAP)
                mine, theirs, ref, n = mo_ref[j], mt_ref[j], sm_ref, half
            systems.append(
                (
                    split(jnp.where(first, mine, theirs)),
                    split(jnp.where(first, theirs, mine)),
                    ref[pl.ds(0, 4 * n), here],
                    ref[pl.ds(4 * n, 3 * n), here],
                    aux_ref[pl.ds(0, 1), lanes],
                    n,
                )
            )
            lengths.append(aux_ref[pl.ds(1, 1), lanes])
            counts.append(float(NODE_MIN * 2 ** (b % LEVELS)))
        vectors = sweeps(systems)
        table = jnp.zeros((8, centres), F32)
        for k, vector in enumerate(vectors):
            _, _, _, geometry, _, n = systems[k]
            rows = wrench_rows(vector, geometry, lengths[k], n, counts[k])
            table = table + pick(rows, slot_ref[pl.ds(k * SLOT_CAP, SLOT_CAP), :], NN)
            if k < len(small):
                xs_ref[:, pl.ds(k * SLOT_CAP, SLOT_CAP)] = vector
            else:
                xm_ref[:, pl.ds((k - len(small)) * SLOT_CAP, SLOT_CAP)] = vector
        t_ref[...] = table

    return call(
        kernel,
        [
            ((4 * quarter, len(small) * SLOT_CAP), F32),
            ((4 * half, len(mid) * SLOT_CAP), F32),
            ((8, centres), F32),
        ],
        values=(*smalls, *mids, sorted_small, sorted_mid, aux, slots),
        flops=1 << 30,
    )


def solve_top(pieces, top, aux, slots, table, buckets, nodes, rows):
    _, _, names = grade(buckets)
    n_low = buckets - len(names)
    width = LEVELS * nodes
    centres = slots.shape[1]
    shares = width // rows
    flat = [p for pair in pieces for side in pair for p in side]

    def kernel(*refs):
        piece_refs = refs[:len(flat)]
        top_ref, aux_ref, slot_ref, tin_ref, x_ref, t_ref, high, low = refs[len(flat):]
        seat = lax.axis_index("gy")
        chip, core = seat // 2, seat % 2
        total = tin_ref[...]
        for k in range(len(names)):
            for side in range(2):
                matrix = core if side == 0 else 1 - core
                for m in range(shares):
                    ref = piece_refs[(k * 2 + side) * shares + m]
                    h, l = split(ref[pl.ds(0, rows), :])
                    place = pl.ds(pl.multiple_of(jnp.bitwise_xor(chip, m) * rows, rows), rows)
                    high[matrix, place, :] = h
                    low[matrix, place, :] = l
            lanes = pl.ds(k * SLOT_CAP, SLOT_CAP)
            aux_lanes = pl.ds((n_low + k) * SLOT_CAP, SLOT_CAP)
            source = top_ref[pl.ds(0, width), lanes]
            geometry = top_ref[pl.ds(width, 3 * nodes), lanes]
            factor = aux_ref[pl.ds(0, 1), aux_lanes]
            length = aux_ref[pl.ds(1, 1), aux_lanes]
            (vector,) = sweeps(
                [((high[0], low[0]), (high[1], low[1]), source, geometry, factor, nodes)]
            )
            x_ref[:, lanes] = vector
            out = wrench_rows(vector, geometry, length, nodes, float(nodes))
            total = total + pick(out, slot_ref[aux_lanes, :], NN)
        t_ref[...] = total

    return call(
        kernel,
        [((width, len(names) * SLOT_CAP), F32), ((8, centres), F32)],
        values=(*flat, top, aux, slots, table),
        scratch=[
            pltpu.VMEM((2, width, width), BF16),
            pltpu.VMEM((2, width, width), BF16),
        ],
        flops=1 << 31,
    )


def unsort(parts, onehot, pieces, nodes, rows):
    fibers = onehot.shape[1]
    spans = [nodes // 4, nodes // 2, nodes]
    own, other = pieces
    chips = len(own)

    def kernel(*refs):
        part_refs, oh_ref = refs[:3], refs[3]
        own_refs, other_refs = refs[4:4 + chips], refs[4 + chips:4 + 2 * chips]
        out_ref, mob_ref = refs[4 + 2 * chips:]
        for c in range(4):
            total, start = None, 0
            for ref, span in zip(part_refs, spans):
                hot = oh_ref[pl.ds(start, ref.shape[1]), :]
                start += ref.shape[1]
                value = pick(ref[pl.ds(c * span, span), :], hot, NN)
                if total is not None:
                    low = total.shape[0]
                    value = jnp.concatenate([value[:low] + total, value[low:]], axis=0)
                total = value
            out_ref[c] = total
        seat = lax.axis_index("gy")
        chip, even = seat // 2, seat % 2 == 0
        lane = lax.broadcasted_iota(jnp.int32, (8, nodes), 1)
        half = nodes // 2
        for m in range(chips):
            place = pl.ds(pl.multiple_of(jnp.bitwise_xor(chip, m) * nodes, nodes), nodes)
            for g in range(mob_ref.shape[0] // 8):
                tile = pl.ds((g // 2) * nodes, nodes)
                mine = own_refs[m][pl.ds(rows, 8), tile]
                theirs = other_refs[m][pl.ds(rows, 8), tile]
                first = jnp.where(even, mine, theirs)
                second = jnp.where(even, theirs, mine)
                if g % 2 == 0:
                    second = pltpu.roll(second, half, 1)
                else:
                    first = pltpu.roll(first, half, 1)
                mob_ref[pl.ds(8 * g, 8), place] = jnp.where(lane < half, first, second)

    return call(
        kernel,
        [((4, nodes, fibers), F32), ((40, chips * nodes), F32)],
        values=(*parts, onehot, *own, *other),
        flops=1 << 28,
    )


def finish(tables, mobility, bucket, attach, offsets, solved, nodes):
    fibers = bucket.shape[1]
    centres = mobility.shape[1]

    def kernel(*refs):
        t_refs = refs[:len(tables)]
        mob_ref, bk_ref, at_ref, off_ref, sol_ref, out_ref, buf, sems = refs[len(tables):]
        copies = [pltpu.make_async_copy(sol_ref.at[3], out_ref.at[3], sems.at[3])]
        copies[0].start()
        table = t_refs[0][...]
        for t in t_refs[1:]:
            table = table + t[...]
        rows = []
        for k in range(6):
            part = mob_ref[pl.ds(6 * k, 6), :] * table[:6]
            rows.append(jnp.sum(part, axis=0, keepdims=True))
        zero = jnp.zeros_like(rows[0])
        motion = jnp.concatenate(rows + [zero, zero], axis=0)
        centre = (
            lax.broadcasted_iota(jnp.int32, (centres, fibers), 0) == at_ref[...]
        ).astype(BF16)
        moving = pick(motion, centre, NN)
        counts = jnp.left_shift(jnp.int32(NODE_MIN), bk_ref[...] % LEVELS)
        mask = lax.broadcasted_iota(jnp.int32, (nodes, fibers), 0) < counts
        u = [moving[k:k + 1] for k in range(3)]
        w = [moving[3 + k:4 + k] for k in range(3)]
        for k, (a, b) in enumerate(((1, 2), (2, 0), (0, 1))):
            rigid = u[k] + (w[a] * off_ref[b] - w[b] * off_ref[a])
            buf[k] = sol_ref[k] + jnp.where(mask, rigid, 0.0)
            copy = pltpu.make_async_copy(buf.at[k], out_ref.at[k], sems.at[k])
            copy.start()
            copies.append(copy)
        for copy in copies:
            copy.wait()

    return call(
        kernel,
        [((4, nodes, fibers), F32)],
        values=(*tables, mobility, bucket, attach, offsets, solved),
        scratch=[pltpu.VMEM((3, nodes, fibers), F32), pltpu.SemaphoreType.DMA((4,))],
        far_out=True,
        flops=1 << 24,
    )[0]


def body(rhs, offsets, lengths, bucket, attach, operator, inverse, mobility):
    nodes, fibers = rhs.shape[1], rhs.shape[2]
    buckets = lax.axis_size("gx")
    seats = lax.axis_size("gy")
    chips = seats // 2
    rows = LEVELS * nodes // chips
    gx = lax.axis_index("gx")
    centres = mobility.shape[1] * seats
    small, mid, top = grade(buckets)

    def hop(value, m):
        return lax.ppermute(value, "gy", [(i, i ^ m) for i in range(seats)])

    def spread(value, source):
        mine = jnp.where(gx == source, value, 0.0)
        for target in range(buckets):
            if target != source:
                got = lax.ppermute(value, "gx", [(source, target)])
                mine = mine + got
        return mine

    share = take_share(operator[0], inverse[0], rows)
    shares = [spread(share, source) for source in top]
    block_mid, block_small, extra = pack_blocks(
        operator[0], inverse[0], mobility, nodes
    )
    shares[0] = jnp.concatenate([shares[0], extra], axis=0)
    mids = jnp.stack([spread(block_mid, source) for source in mid])
    smalls = [block_small]
    for shift in range(1, buckets):
        smalls.append(lax.ppermute(block_small, "gx", [(s, (s - shift) % buckets) for s in small]))
    smalls = jnp.stack(smalls)

    bucket_row = bucket.reshape(1, fibers)
    attach_row = attach.reshape(1, fibers)
    onehot, slots, sorted_small, sorted_mid, sorted_top, aux = sort_fibers(
        bucket_row, attach_row, lengths.reshape(1, fibers), rhs, offsets,
        buckets, centres, nodes,
    )

    pieces = []
    for mine in shares:
        own = [mine] + [hop(mine, 2 * m) for m in range(1, chips)]
        other = [hop(piece, 1) for piece in own]
        pieces.append((own, other))

    other_mids = hop(mids, 1)
    other_smalls = hop(smalls, 1)
    x_small, x_mid, table_low = solve_low(
        (smalls, other_smalls), (mids, other_mids), sorted_small, sorted_mid,
        aux, slots, buckets, nodes,
    )
    x_top, table = solve_top(pieces, sorted_top, aux, slots, table_low, buckets, nodes, rows)

    table = table + hop(table, 1)
    tables = [table] + [hop(table, 2 * m) for m in range(1, chips)]
    solved, mobility_all = unsort(
        (x_small, x_mid, x_top), onehot, pieces[0], nodes, rows
    )
    return finish(tables, mobility_all, bucket_row, attach_row, offsets, solved, nodes)


def solution(mesh):
    in_specs = (
        P(None, None, ("gx", "gy")),
        P(None, None, ("gx", "gy")),
        P(("gx", "gy")),
        P(("gx", "gy"), None),
        P(("gx", "gy")),
        P("gx", None, None),
        P("gx", None, None),
        P(None, ("gx", "gy")),
    )
    out_specs = P(None, None, ("gx", "gy"))
    return jax.shard_map(body, mesh=mesh, in_specs=in_specs, out_specs=out_specs, check_vma=False)
```

profile of v0, /device:TPU:0, one launch (start us, length us, event | category | flops | bytes accessed | tf_op | source)
XLA Modules:
  0.0 63.1 jit_solution(677369644172759038)
XLA Ops:
  0.0 1.2 %copy-done = f32[1,512,512]{2,1,0:T(8,128)S(1)} copy-done((f32[1,512,512]{2,1,0:T(8,128)S(1)}, f32[1,512,512]{2,1,0:T(8,128)}, u32[]{:S(2)}) %copy-start) | copy-done | bytes 1048600
  1.2 1.2 %copy-done.1 = f32[1,512,512]{2,1,0:T(8,128)S(1)} copy-done((f32[1,512,512]{2,1,0:T(8,128)S(1)}, f32[1,512,512]{2,1,0:T(8,128)}, u32[]{:S(2)}) %copy-start.1) | copy-done | bytes 1048600
  2.5 1.3 %collective-permute-start = (f32[128,512]{1,0:T(8,128)S(1)}, f32[128,512]{1,0:T(8,128)S(1)}, u32[]{:S(2)}, u32[]{:S(2)}) collective-permute-start(f32[128,512]{1,0:T(8,128)S(1)} %shard_map.82), channel_id=1, source_target_pairs={{24,0},{25,1},{26,2},{27,3},{28,4},{29,5},{30,6},{31,7}} | collective-permute-start | bytes 786440 | tf_op jit(solution)/shard_map/ppermute | solution.py:469
  3.8 0.7 %collective-permute-start.1 = (f32[128,512]{1,0:T(8,128)S(1)}, f32[128,512]{1,0:T(8,128)S(1)}, u32[]{:S(2)}, u32[]{:S(2)}) collective-permute-start(f32[128,512]{1,0:T(8,128)S(1)} %shard_map.82), channel_id=1, source_target_pairs={{24,8},{25,9},{26,10},{27,11},{28,12},{29,13},{30,14},{31,15}} | collective-permute-start | bytes 786440 | tf_op jit(solution)/shard_map/ppermute | solution.py:469
  4.5 0.7 %collective-permute-start.2 = (f32[128,512]{1,0:T(8,128)S(1)}, f32[128,512]{1,0:T(8,128)S(1)}, u32[]{:S(2)}, u32[]{:S(2)}) collective-permute-start(f32[128,512]{1,0:T(8,128)S(1)} %shard_map.82), channel_id=1, source_target_pairs={{24,16},{25,17},{26,18},{27,19},{28,20},{29,21},{30,22},{31,23}} | collective-permute-start | bytes 786440 | tf_op jit(solution)/shard_map/ppermute | solution.py:469
  5.2 0.9 %shard_map.83 = (f32[256,256]{1,0:T(8,128)S(1)}, f32[128,128]{1,0:T(8,128)S(1)}, f32[8,512]{1,0:T(8,128)S(1)}) custom-call(f32[512,512]{1,0:T(8,128)S(1)} %bitcast.12, f32[512,512]{1,0:T(8,128)S(1)} %bitcast.14, f32[36,64]{1,0:T(8,128)S(1)} %copy-done.3), custom_call_target="tpu_custom_call" | custom-call | flops 1048576 | bytes 1048576 | tf_op jit(solution)/shard_map/pallas_call | solution.py:48
  6.1 8.6 %collective-permute-start.10 = (f32[128,128]{1,0:T(8,128)S(1)}, f32[128,128]{1,0:T(8,128)S(1)}, u32[]{:S(2)}, u32[]{:S(2)}) collective-permute-start(f32[128,128]{1,0:T(8,128)S(1)} %get-tuple-element.25), channel_id=1, source_target_pairs={{0,24},{8,0},{1,25},{9,1},{2,26},{10,2},{3,27},{11,3},{4,28},{12,4... | collective-permute-start | bytes 196616 | tf_op jit(solution)/shard_map/ppermute | solution.py:482
  14.7 1.3 %collective-permute-start.11 = (f32[128,128]{1,0:T(8,128)S(1)}, f32[128,128]{1,0:T(8,128)S(1)}, u32[]{:S(2)}, u32[]{:S(2)}) collective-permute-start(f32[128,128]{1,0:T(8,128)S(1)} %get-tuple-element.25), channel_id=1, source_target_pairs={{0,16},{8,24},{1,17},{9,25},{2,18},{10,26},{3,19},{11,27},{4,20},{... | collective-permute-start | bytes 196616 | tf_op jit(solution)/shard_map/ppermute | solution.py:482
  16.0 1.1 %collective-permute-done.10 = f32[128,128]{1,0:T(8,128)S(1)} collective-permute-done((f32[128,128]{1,0:T(8,128)S(1)}, f32[128,128]{1,0:T(8,128)S(1)}, u32[]{:S(2)}, u32[]{:S(2)}) %collective-permute-start.10) | collective-permute-done | bytes 65568 | tf_op jit(solution)/shard_map/ppermute | solution.py:482
  17.1 1.4 %collective-permute-start.12 = (f32[128,128]{1,0:T(8,128)S(1)}, f32[128,128]{1,0:T(8,128)S(1)}, u32[]{:S(2)}, u32[]{:S(2)}) collective-permute-start(f32[128,128]{1,0:T(8,128)S(1)} %get-tuple-element.25), channel_id=1, source_target_pairs={{0,8},{8,16},{1,9},{9,17},{2,10},{10,18},{3,11},{11,19},{4,12},{12... | collective-permute-start | bytes 196616 | tf_op jit(solution)/shard_map/ppermute | solution.py:482
  18.5 0.0 collective-permute-done.11
  18.5 1.3 %collective-permute-start.14 = (f32[256,256]{1,0:T(8,128)S(1)}, f32[256,256]{1,0:T(8,128)S(1)}, u32[]{:S(2)}, u32[]{:S(2)}) collective-permute-start(f32[256,256]{1,0:T(8,128)S(1)} %get-tuple-element.26), channel_id=1, source_target_pairs={{16,0},{17,1},{18,2},{19,3},{20,4},{21,5},{22,6},{23,7}} | collective-permute-start | bytes 786440 | tf_op jit(solution)/shard_map/ppermute | solution.py:469
  19.8 0.6 collective-permute-done.12
  20.4 0.7 %collective-permute-start.15 = (f32[256,256]{1,0:T(8,128)S(1)}, f32[256,256]{1,0:T(8,128)S(1)}, u32[]{:S(2)}, u32[]{:S(2)}) collective-permute-start(f32[256,256]{1,0:T(8,128)S(1)} %get-tuple-element.26), channel_id=1, source_target_pairs={{16,8},{17,9},{18,10},{19,11},{20,12},{21,13},{22,14},{23,15}} | collective-permute-start | bytes 786440 | tf_op jit(solution)/shard_map/ppermute | solution.py:469
  21.1 0.0 collective-permute-done
  21.1 0.7 %collective-permute-start.16 = (f32[256,256]{1,0:T(8,128)S(1)}, f32[256,256]{1,0:T(8,128)S(1)}, u32[]{:S(2)}, u32[]{:S(2)}) collective-permute-start(f32[256,256]{1,0:T(8,128)S(1)} %get-tuple-element.26), channel_id=1, source_target_pairs={{16,24},{17,25},{18,26},{19,27},{20,28},{21,29},{22,30},{23,31}} | collective-permute-start | bytes 786440 | tf_op jit(solution)/shard_map/ppermute | solution.py:469
  21.8 0.1 collective-permute-start.13
  21.8 0.0 collective-permute-done.2
  21.9 0.1 add_add_fusion
  22.0 0.0 copy-start.6
  22.0 0.0 copy-start.2
  22.0 2.1 %collective-permute-start.3 = (f32[136,512]{1,0:T(8,128)S(1)}, f32[136,512]{1,0:T(8,128)S(1)}, u32[]{:S(2)}, u32[]{:S(2)}) collective-permute-start(f32[136,512]{1,0:T(8,128)S(1)} %pad_maximum_fusion.refs_0_.refs_4_), channel_id=1, source_target_pairs={{0,2},{1,3},{2,0},{3,1},{4,6},{5,7},{6,4},{7,5},{8,10},{9,11},{10,... | collective-permute-start | bytes 835592 | tf_op jit(solution)/shard_map/ppermute | solution.py:463
  24.1 6.4 %collective-permute-done.14 = f32[256,256]{1,0:T(8,128)S(1)} collective-permute-done((f32[256,256]{1,0:T(8,128)S(1)}, f32[256,256]{1,0:T(8,128)S(1)}, u32[]{:S(2)}, u32[]{:S(2)}) %collective-permute-start.14) | collective-permute-done | bytes 262176 | tf_op jit(solution)/shard_map/ppermute | solution.py:469
  30.5 2.0 %collective-permute-start.4 = (f32[136,512]{1,0:T(8,128)S(1)}, f32[136,512]{1,0:T(8,128)S(1)}, u32[]{:S(2)}, u32[]{:S(2)}) collective-permute-start(f32[136,512]{1,0:T(8,128)S(1)} %pad_maximum_fusion.refs_0_.refs_4_), channel_id=1, source_target_pairs={{0,4},{1,5},{2,6},{3,7},{4,0},{5,1},{6,2},{7,3},{8,12},{9,13},{10,... | collective-permute-start | bytes 835592 | tf_op jit(solution)/shard_map/ppermute | solution.py:463
  32.5 1.4 %collective-permute-start.5 = (f32[136,512]{1,0:T(8,128)S(1)}, f32[136,512]{1,0:T(8,128)S(1)}, u32[]{:S(2)}, u32[]{:S(2)}) collective-permute-start(f32[136,512]{1,0:T(8,128)S(1)} %pad_maximum_fusion.refs_0_.refs_4_), channel_id=1, source_target_pairs={{0,6},{1,7},{2,4},{3,5},{4,2},{5,3},{6,0},{7,1},{8,14},{9,15},{10,... | collective-permute-start | bytes 835592 | tf_op jit(solution)/shard_map/ppermute | solution.py:463
  33.9 0.0 collective-permute-done.16
  33.9 0.1 add_bitcast_fusion.mo_ref
  34.0 0.1 collective-permute-start.17
  34.1 0.5 collective-permute-start.6
  34.6 0.0 collective-permute-done.3.refs_1_.refs_5_
  34.6 0.1 collective-permute-start.7
  34.7 7.6 %collective-permute-done.4.refs_2_.refs_6_ = f32[136,512]{1,0:T(8,128)S(1)} collective-permute-done((f32[136,512]{1,0:T(8,128)S(1)}, f32[136,512]{1,0:T(8,128)S(1)}, u32[]{:S(2)}, u32[]{:S(2)}) %collective-permute-start.4) | collective-permute-done | bytes 278560 | tf_op jit(solution)/shard_map/ppermute | solution.py:463
  42.3 0.5 collective-permute-start.9
  42.8 0.7 %copy-done.4 = s32[512,1]{0,1:T(1,128)S(1)} copy-done((s32[512,1]{0,1:T(1,128)S(1)}, s32[512,1]{0,1:T(1,128)}, u32[]{:S(2)}) %copy-start.4) | copy-done | bytes 2072
  43.5 3.1 %shard_map.84 = (bf16[512,512]{1,0:T(8,128)(2,1)S(1)}, bf16[512,512]{1,0:T(8,128)(2,1)S(1)}, f32[224,256]{1,0:T(8,128)S(1)}, f32[448,128]{1,0:T(8,128)S(1)}, f32...) custom-call(s32[1,512]{1,0:T(1,128)S(1)} %bitcast.16, s32[1,512]{1,0:T(1,128)S(1)} %bitcast.18, f32[1,512]{1,0:T(1,128)S(1)} %bitcast.20, ...), custom_call_target="tpu_custom_call" | custom-call | flops 1073741824 | bytes 1048576 | tf_op jit(solution)/shard_map/pallas_call | solution.py:48
  46.6 2.2 %shard_map.85 = (f32[128,256]{1,0:T(8,128)S(1)}, f32[256,128]{1,0:T(8,128)S(1)}, f32[8,512]{1,0:T(8,128)S(1)}) custom-call(f32[4,128,128]{2,1,0:T(8,128)S(1)} %pad_maximum_fusion.1.so_ref, f32[4,128,128]{2,1,0:T(8,128)S(1)} %collective-permute-done.13.st_ref, f32[1,256,256]{2,1,0:T(8,128)S(1)} %add_bitcast_fusion.mo_ref, ...), custom_call_target="tpu_custom_call" | custom-call | flops 1073741824 | bytes 1048576 | tf_op jit(solution)/shard_map/pallas_call | solution.py:48
  48.7 0.0 collective-permute-done.6.refs_4_.refs_8_
  48.7 0.0 collective-permute-done.7.refs_5_.refs_9_
  48.8 0.0 collective-permute-done.8.refs_6_.refs_10_
  48.8 3.8 %shard_map.86 = (f32[512,128]{1,0:T(8,128)S(1)}, f32[8,512]{1,0:T(8,128)S(1)}) custom-call(f32[136,512]{1,0:T(8,128)S(1)} %pad_maximum_fusion.refs_0_.refs_4_, f32[136,512]{1,0:T(8,128)S(1)} %collective-permute-done.3.refs_1_.refs_5_, f32[136,512]{1,0:T(8,128)S(1)} %collective-permute-done.4.refs_2_.refs_6_, ...), custom_call_target="tpu_custom_call" | custom-call | flops 2147483648 | bytes 1048576 | tf_op jit(solution)/shard_map/pallas_call | solution.py:48
  52.6 1.2 %collective-permute-done.18 = f32[8,512]{1,0:T(8,128)S(1)} collective-permute-done((f32[8,512]{1,0:T(8,128)S(1)}, f32[8,512]{1,0:T(8,128)S(1)}, u32[]{:S(2)}, u32[]{:S(2)}) %collective-permute-start.18) | collective-permute-done | bytes 16416 | tf_op jit(solution)/shard_map/ppermute | solution.py:463
  53.8 1.7 %collective-permute-start.19 = (f32[8,512]{1,0:T(8,128)S(1)}, f32[8,512]{1,0:T(8,128)S(1)}, u32[]{:S(2)}, u32[]{:S(2)}) collective-permute-start(f32[8,512]{1,0:T(8,128)S(1)} %add.27.refs_0_), channel_id=1, source_target_pairs={{0,2},{1,3},{2,0},{3,1},{4,6},{5,7},{6,4},{7,5},{8,10},{9,11},{10,... | collective-permute-start | bytes 49160 | tf_op jit(solution)/shard_map/ppermute | solution.py:463
  55.5 1.5 %collective-permute-start.20 = (f32[8,512]{1,0:T(8,128)S(1)}, f32[8,512]{1,0:T(8,128)S(1)}, u32[]{:S(2)}, u32[]{:S(2)}) collective-permute-start(f32[8,512]{1,0:T(8,128)S(1)} %add.27.refs_0_), channel_id=1, source_target_pairs={{0,4},{1,5},{2,6},{3,7},{4,0},{5,1},{6,2},{7,3},{8,12},{9,13},{10,... | collective-permute-start | bytes 49160 | tf_op jit(solution)/shard_map/ppermute | solution.py:463
  57.0 0.3 collective-permute-start.21
  57.3 0.9 %shard_map.87 = (f32[4,128,512]{2,1,0:T(8,128)S(1)}, f32[40,512]{1,0:T(8,128)S(1)}) custom-call(f32[128,256]{1,0:T(8,128)S(1)} %get-tuple-element.31.refs_0_, f32[256,128]{1,0:T(8,128)S(1)} %get-tuple-element.32.refs_1_, f32[512,128]{1,0:T(8,128)S(1)} %get-tuple-element.33.refs_2_, bf16[512,512]{1,0:T(8,128)(2,1)S(1)} %get-tuple-element.34.refs_3_, ...), custom_call_target="tpu_custom_call" | custom-call | flops 268435456 | bytes 1048576 | tf_op jit(solution)/shard_map/pallas_call | solution.py:48
  58.2 1.0 %collective-permute-done.20.refs_2_ = f32[8,512]{1,0:T(8,128)S(1)} collective-permute-done((f32[8,512]{1,0:T(8,128)S(1)}, f32[8,512]{1,0:T(8,128)S(1)}, u32[]{:S(2)}, u32[]{:S(2)}) %collective-permute-start.20) | collective-permute-done | bytes 16416 | tf_op jit(solution)/shard_map/ppermute | solution.py:463
  59.2 2.4 %collective-permute-done.21.refs_3_ = f32[8,512]{1,0:T(8,128)S(1)} collective-permute-done((f32[8,512]{1,0:T(8,128)S(1)}, f32[8,512]{1,0:T(8,128)S(1)}, u32[]{:S(2)}, u32[]{:S(2)}) %collective-permute-start.21) | collective-permute-done | bytes 16416 | tf_op jit(solution)/shard_map/ppermute | solution.py:463
  61.6 1.5 %shard_map.88 = f32[4,128,512]{2,1,0:T(8,128)} custom-call(f32[8,512]{1,0:T(8,128)S(1)} %add.27.refs_0_, f32[8,512]{1,0:T(8,128)S(1)} %collective-permute-done.19.refs_1_, f32[8,512]{1,0:T(8,128)S(1)} %collective-permute-done.20.refs_2_, f32[8,512]{1,0:T(8,128)S(1)} %collective-permute-done.21.refs_3_, f32[40,512]{1,0:T(8,128)S(1)} %get-tuple-element.35.refs_4_, ...), custom_call_target="tpu_custom_call" | custom-call | flops 16777216 | bytes 1048576 | tf_op jit(solution)/shard_map/pallas_call | solution.py:48
  (24 shorter events, 0.1 us)
Async XLA Ops:
  0.0 1.2 %copy-start = (f32[1,512,512]{2,1,0:T(8,128)S(1)}, f32[1,512,512]{2,1,0:T(8,128)}, u32[]{:S(2)}) copy-start(f32[1,512,512]{2,1,0:T(8,128)} %param.13) | copy-start | bytes 3145732
  1.2 1.2 %copy-start.1 = (f32[1,512,512]{2,1,0:T(8,128)S(1)}, f32[1,512,512]{2,1,0:T(8,128)}, u32[]{:S(2)}) copy-start(f32[1,512,512]{2,1,0:T(8,128)} %param.14) | copy-start | bytes 3145732
  2.5 2.7 %copy-start.3 = (f32[36,64]{1,0:T(8,128)S(1)}, f32[36,64]{1,0:T(8,128)}, u32[]{:S(2)}) copy-start(f32[36,64]{1,0:T(8,128)} %mob_ref.1) | copy-start | bytes 27652
  2.5 18.6 %collective-permute-start = (f32[128,512]{1,0:T(8,128)S(1)}, f32[128,512]{1,0:T(8,128)S(1)}, u32[]{:S(2)}, u32[]{:S(2)}) collective-permute-start(f32[128,512]{1,0:T(8,128)S(1)} %shard_map.82), channel_id=1, source_target_pairs={{24,0},{25,1},{26,2},{27,3},{28,4},{29,5},{30,6},{31,7}} | collective-permute-start | bytes 786440 | tf_op jit(solution)/shard_map/ppermute | solution.py:469
  3.8 18.0 %collective-permute-start.1 = (f32[128,512]{1,0:T(8,128)S(1)}, f32[128,512]{1,0:T(8,128)S(1)}, u32[]{:S(2)}, u32[]{:S(2)}) collective-permute-start(f32[128,512]{1,0:T(8,128)S(1)} %shard_map.82), channel_id=1, source_target_pairs={{24,8},{25,9},{26,10},{27,11},{28,12},{29,13},{30,14},{31,15}} | collective-permute-start | bytes 786440 | tf_op jit(solution)/shard_map/ppermute | solution.py:469
  4.5 17.4 %collective-permute-start.2 = (f32[128,512]{1,0:T(8,128)S(1)}, f32[128,512]{1,0:T(8,128)S(1)}, u32[]{:S(2)}, u32[]{:S(2)}) collective-permute-start(f32[128,512]{1,0:T(8,128)S(1)} %shard_map.82), channel_id=1, source_target_pairs={{24,16},{25,17},{26,18},{27,19},{28,20},{29,21},{30,22},{31,23}} | collective-permute-start | bytes 786440 | tf_op jit(solution)/shard_map/ppermute | solution.py:469
  6.1 11.0 %collective-permute-start.10 = (f32[128,128]{1,0:T(8,128)S(1)}, f32[128,128]{1,0:T(8,128)S(1)}, u32[]{:S(2)}, u32[]{:S(2)}) collective-permute-start(f32[128,128]{1,0:T(8,128)S(1)} %get-tuple-element.25), channel_id=1, source_target_pairs={{0,24},{8,0},{1,25},{9,1},{2,26},{10,2},{3,27},{11,3},{4,28},{12,4... | collective-permute-start | bytes 196616 | tf_op jit(solution)/shard_map/ppermute | solution.py:482
  14.7 3.8 %collective-permute-start.11 = (f32[128,128]{1,0:T(8,128)S(1)}, f32[128,128]{1,0:T(8,128)S(1)}, u32[]{:S(2)}, u32[]{:S(2)}) collective-permute-start(f32[128,128]{1,0:T(8,128)S(1)} %get-tuple-element.25), channel_id=1, source_target_pairs={{0,16},{8,24},{1,17},{9,25},{2,18},{10,26},{3,19},{11,27},{4,20},{... | collective-permute-start | bytes 196616 | tf_op jit(solution)/shard_map/ppermute | solution.py:482
  17.1 3.3 %collective-permute-start.12 = (f32[128,128]{1,0:T(8,128)S(1)}, f32[128,128]{1,0:T(8,128)S(1)}, u32[]{:S(2)}, u32[]{:S(2)}) collective-permute-start(f32[128,128]{1,0:T(8,128)S(1)} %get-tuple-element.25), channel_id=1, source_target_pairs={{0,8},{8,16},{1,9},{9,17},{2,10},{10,18},{3,11},{11,19},{4,12},{12... | collective-permute-start | bytes 196616 | tf_op jit(solution)/shard_map/ppermute | solution.py:482
  18.5 12.0 %collective-permute-start.14 = (f32[256,256]{1,0:T(8,128)S(1)}, f32[256,256]{1,0:T(8,128)S(1)}, u32[]{:S(2)}, u32[]{:S(2)}) collective-permute-start(f32[256,256]{1,0:T(8,128)S(1)} %get-tuple-element.26), channel_id=1, source_target_pairs={{16,0},{17,1},{18,2},{19,3},{20,4},{21,5},{22,6},{23,7}} | collective-permute-start | bytes 786440 | tf_op jit(solution)/shard_map/ppermute | solution.py:469
  20.4 12.1 %collective-permute-start.15 = (f32[256,256]{1,0:T(8,128)S(1)}, f32[256,256]{1,0:T(8,128)S(1)}, u32[]{:S(2)}, u32[]{:S(2)}) collective-permute-start(f32[256,256]{1,0:T(8,128)S(1)} %get-tuple-element.26), channel_id=1, source_target_pairs={{16,8},{17,9},{18,10},{19,11},{20,12},{21,13},{22,14},{23,15}} | collective-permute-start | bytes 786440 | tf_op jit(solution)/shard_map/ppermute | solution.py:469
  21.1 12.9 %collective-permute-start.16 = (f32[256,256]{1,0:T(8,128)S(1)}, f32[256,256]{1,0:T(8,128)S(1)}, u32[]{:S(2)}, u32[]{:S(2)}) collective-permute-start(f32[256,256]{1,0:T(8,128)S(1)} %get-tuple-element.26), channel_id=1, source_target_pairs={{16,24},{17,25},{18,26},{19,27},{20,28},{21,29},{22,30},{23,31}} | collective-permute-start | bytes 786440 | tf_op jit(solution)/shard_map/ppermute | solution.py:469
  21.8 12.3 %collective-permute-start.13 = (f32[4,128,128]{2,1,0:T(8,128)S(1)}, f32[4,128,128]{2,1,0:T(8,128)S(1)}, u32[]{:S(2)}, u32[]{:S(2)}) collective-permute-start(f32[4,128,128]{2,1,0:T(8,128)S(1)} %pad_maximum_fusion.1.so_ref), channel_id=1, source_target_pairs={{0,1},{1,0},{2,3},{3,2},{4,5},{5,4},{6,7},{7,6},{8,9},{9,8},{10,11... | collective-permute-start | bytes 786440 | tf_op jit(solution)/shard_map/ppermute | solution.py:463
  22.0 20.9 %copy-start.6 = (f32[4,128,512]{2,1,0:T(8,128)S(1)}, f32[4,128,512]{2,1,0:T(8,128)}, u32[]{:S(2)}) copy-start(f32[4,128,512]{2,1,0:T(8,128)} %rhs_ref.1) | copy-start | bytes 3145732
  22.0 20.8 %copy-start.2 = (f32[3,128,512]{2,1,0:T(8,128)S(1)}, f32[3,128,512]{2,1,0:T(8,128)}, u32[]{:S(2)}) copy-start(f32[3,128,512]{2,1,0:T(8,128)} %refs_7_.1) | copy-start | bytes 2359300
  22.0 12.6 %collective-permute-start.3 = (f32[136,512]{1,0:T(8,128)S(1)}, f32[136,512]{1,0:T(8,128)S(1)}, u32[]{:S(2)}, u32[]{:S(2)}) collective-permute-start(f32[136,512]{1,0:T(8,128)S(1)} %pad_maximum_fusion.refs_0_.refs_4_), channel_id=1, source_target_pairs={{0,2},{1,3},{2,0},{3,1},{4,6},{5,7},{6,4},{7,5},{8,10},{9,11},{10,... | collective-permute-start | bytes 835592 | tf_op jit(solution)/shard_map/ppermute | solution.py:463
  30.5 11.8 %collective-permute-start.4 = (f32[136,512]{1,0:T(8,128)S(1)}, f32[136,512]{1,0:T(8,128)S(1)}, u32[]{:S(2)}, u32[]{:S(2)}) collective-permute-start(f32[136,512]{1,0:T(8,128)S(1)} %pad_maximum_fusion.refs_0_.refs_4_), channel_id=1, source_target_pairs={{0,4},{1,5},{2,6},{3,7},{4,0},{5,1},{6,2},{7,3},{8,12},{9,13},{10,... | collective-permute-start | bytes 835592 | tf_op jit(solution)/shard_map/ppermute | solution.py:463
  32.5 9.8 %collective-permute-start.5 = (f32[136,512]{1,0:T(8,128)S(1)}, f32[136,512]{1,0:T(8,128)S(1)}, u32[]{:S(2)}, u32[]{:S(2)}) collective-permute-start(f32[136,512]{1,0:T(8,128)S(1)} %pad_maximum_fusion.refs_0_.refs_4_), channel_id=1, source_target_pairs={{0,6},{1,7},{2,4},{3,5},{4,2},{5,3},{6,0},{7,1},{8,14},{9,15},{10,... | collective-permute-start | bytes 835592 | tf_op jit(solution)/shard_map/ppermute | solution.py:463
  33.9 8.9 %copy-start.5 = (s32[512]{0:T(512)S(1)}, s32[512]{0:T(512)}, u32[]{:S(2)}) copy-start(s32[512]{0:T(512)} %param.12) | copy-start | bytes 6148
  33.9 8.9 %copy-start.7 = (f32[512]{0:T(512)S(1)}, f32[512]{0:T(512)}, u32[]{:S(2)}) copy-start(f32[512]{0:T(512)} %param.10) | copy-start | bytes 6148
  34.0 12.6 %collective-permute-start.17 = (f32[1,256,256]{2,1,0:T(8,128)S(1)}, f32[1,256,256]{2,1,0:T(8,128)S(1)}, u32[]{:S(2)}, u32[]{:S(2)}) collective-permute-start(f32[1,256,256]{2,1,0:T(8,128)S(1)} %add_bitcast_fusion.mo_ref), channel_id=1, source_target_pairs={{0,1},{1,0},{2,3},{3,2},{4,5},{5,4},{6,7},{7,6},{8,9},{9,8},{10,11... | collective-permute-start | bytes 786440 | tf_op jit(solution)/shard_map/ppermute | solution.py:463
  34.1 14.6 %collective-permute-start.6 = (f32[136,512]{1,0:T(8,128)S(1)}, f32[136,512]{1,0:T(8,128)S(1)}, u32[]{:S(2)}, u32[]{:S(2)}) collective-permute-start(f32[136,512]{1,0:T(8,128)S(1)} %pad_maximum_fusion.refs_0_.refs_4_), channel_id=1, source_target_pairs={{0,1},{1,0},{2,3},{3,2},{4,5},{5,4},{6,7},{7,6},{8,9},{9,8},{10,11... | collective-permute-start | bytes 835592 | tf_op jit(solution)/shard_map/ppermute | solution.py:463
  34.6 14.1 %collective-permute-start.7 = (f32[136,512]{1,0:T(8,128)S(1)}, f32[136,512]{1,0:T(8,128)S(1)}, u32[]{:S(2)}, u32[]{:S(2)}) collective-permute-start(f32[136,512]{1,0:T(8,128)S(1)} %collective-permute-done.3.refs_1_.refs_5_), channel_id=1, source_target_pairs={{0,1},{1,0},{2,3},{3,2},{4,5},{5,4},{6,7},{7,6},{8,9},{9,8},{10,11... | collective-permute-start | bytes 835592 | tf_op jit(solution)/shard_map/ppermute | solution.py:463
  42.3 6.5 %collective-permute-start.8 = (f32[136,512]{1,0:T(8,128)S(1)}, f32[136,512]{1,0:T(8,128)S(1)}, u32[]{:S(2)}, u32[]{:S(2)}) collective-permute-start(f32[136,512]{1,0:T(8,128)S(1)} %collective-permute-done.4.refs_2_.refs_6_), channel_id=1, source_target_pairs={{0,1},{1,0},{2,3},{3,2},{4,5},{5,4},{6,7},{7,6},{8,9},{9,8},{10,11... | collective-permute-start | bytes 835592 | tf_op jit(solution)/shard_map/ppermute | solution.py:463
  42.3 6.5 %collective-permute-start.9 = (f32[136,512]{1,0:T(8,128)S(1)}, f32[136,512]{1,0:T(8,128)S(1)}, u32[]{:S(2)}, u32[]{:S(2)}) collective-permute-start(f32[136,512]{1,0:T(8,128)S(1)} %collective-permute-done.5.refs_3_.refs_7_), channel_id=1, source_target_pairs={{0,1},{1,0},{2,3},{3,2},{4,5},{5,4},{6,7},{7,6},{8,9},{9,8},{10,11... | collective-permute-start | bytes 835592 | tf_op jit(solution)/shard_map/ppermute | solution.py:463
  42.8 0.7 %copy-start.4 = (s32[512,1]{0,1:T(1,128)S(1)}, s32[512,1]{0,1:T(1,128)}, u32[]{:S(2)}) copy-start(s32[512,1]{0,1:T(1,128)} %param.11) | copy-start | bytes 6148
  52.5 1.2 %collective-permute-start.18 = (f32[8,512]{1,0:T(8,128)S(1)}, f32[8,512]{1,0:T(8,128)S(1)}, u32[]{:S(2)}, u32[]{:S(2)}) collective-permute-start(f32[8,512]{1,0:T(8,128)S(1)} %get-tuple-element.30), channel_id=1, source_target_pairs={{0,1},{1,0},{2,3},{3,2},{4,5},{5,4},{6,7},{7,6},{8,9},{9,8},{10,11... | collective-permute-start | bytes 49160 | tf_op jit(solution)/shard_map/ppermute | solution.py:463
  53.8 4.4 %collective-permute-start.19 = (f32[8,512]{1,0:T(8,128)S(1)}, f32[8,512]{1,0:T(8,128)S(1)}, u32[]{:S(2)}, u32[]{:S(2)}) collective-permute-start(f32[8,512]{1,0:T(8,128)S(1)} %add.27.refs_0_), channel_id=1, source_target_pairs={{0,2},{1,3},{2,0},{3,1},{4,6},{5,7},{6,4},{7,5},{8,10},{9,11},{10,... | collective-permute-start | bytes 49160 | tf_op jit(solution)/shard_map/ppermute | solution.py:463
  55.5 3.7 %collective-permute-start.20 = (f32[8,512]{1,0:T(8,128)S(1)}, f32[8,512]{1,0:T(8,128)S(1)}, u32[]{:S(2)}, u32[]{:S(2)}) collective-permute-start(f32[8,512]{1,0:T(8,128)S(1)} %add.27.refs_0_), channel_id=1, source_target_pairs={{0,4},{1,5},{2,6},{3,7},{4,0},{5,1},{6,2},{7,3},{8,12},{9,13},{10,... | collective-permute-start | bytes 49160 | tf_op jit(solution)/shard_map/ppermute | solution.py:463
  57.0 4.6 %collective-permute-start.21 = (f32[8,512]{1,0:T(8,128)S(1)}, f32[8,512]{1,0:T(8,128)S(1)}, u32[]{:S(2)}, u32[]{:S(2)}) collective-permute-start(f32[8,512]{1,0:T(8,128)S(1)} %add.27.refs_0_), channel_id=1, source_target_pairs={{0,6},{1,7},{2,4},{3,5},{4,2},{5,3},{6,0},{7,1},{8,14},{9,15},{10,... | collective-permute-start | bytes 49160 | tf_op jit(solution)/shard_map/ppermute | solution.py:463
where the time goes:
time: 63.5 us; the launch traced here: 63.1 us
  starting transfers between devices  26.8 us (42%)
  waiting for transfers between devices  20.4 us (32%)
  Pallas kernels  12.3 us (19%)
  local copies, waits for them, and re-layouts  3.13 us (5%)
    pallas_call x7, Pallas kernels, call(): pl.pallas_call(kernel, out_shape=out_shape, in_specs=[ANY] * len(far) + [...  12.3 us
    ppermute x13, waiting for transfers between devices, hop(): return lax.ppermute(value, 'gy', [(i, i ^ m) for i in range(seats)])  12.3 us
    ppermute x3, starting transfers between devices, body(): lax.ppermute(block_small, 'gx', [(s, (s - shift) % buckets) for s in small])  11.3 us
    ppermute x13, starting transfers between devices, hop(): return lax.ppermute(value, 'gy', [(i, i ^ m) for i in range(seats)])  10.3 us
    ppermute x6, waiting for transfers between devices, spread(): got = lax.ppermute(value, 'gx', [(source, target)])  6.39 us
    ppermute x6, starting transfers between devices, spread(): got = lax.ppermute(value, 'gx', [(source, target)])  5.28 us
    unnamed x16, local copies, waits for them, and re-layouts  3.13 us
    ppermute x3, waiting for transfers between devices, body(): lax.ppermute(block_small, 'gx', [(s, (s - shift) % buckets) for s in small])  1.67 us
  transfers between devices with their start and end apart: 22, of which 7 were waited for; matrix products, arithmetic and copies ran while one was open for 0% of the time, Pallas kernels for 11%

commit v1 on v0

--- a/solution.py
+++ b/solution.py
@@ -10,6 +10,7 @@
 LEVELS = 4
 ITERS = 4
 SLOT_CAP = 128
+CHUNKS = 2
 VMEM_LIMIT = 32 << 20
 F32 = jnp.float32
 BF16 = jnp.bfloat16
@@ -33,6 +34,7 @@
 
 
 VM = pl.BlockSpec(memory_space=pltpu.VMEM)
+FAR = pl.BlockSpec(memory_space=pltpu.HBM)
 ANY = pl.BlockSpec(memory_space=pl.ANY)
 
 
@@ -48,24 +50,34 @@
     return pl.pallas_call(
         kernel,
         out_shape=out_shape,
-        in_specs=[ANY] * len(far) + [VM] * len(values),
+        in_specs=[FAR] * len(far) + [VM] * len(values),
         out_specs=tuple(ANY if far_out else VM for _ in outs),
         scratch_shapes=list(scratch),
         compiler_params=pltpu.CompilerParams(vmem_limit_bytes=VMEM_LIMIT),
         cost_estimate=pl.CostEstimate(flops=flops, transcendentals=0, bytes_accessed=1 << 20),
-    )(*far, *near(*values))
+    )(*(pltpu.with_memory_space_constraint(v, pltpu.HBM) for v in far), *near(*values))
 
 
 def take_share(operator, inverse, rows):
     width = operator.shape[1]
 
-    def kernel(op_ref, inv_ref, a_ref, sem):
+    part = rows // CHUNKS
+
+    def kernel(op_ref, inv_ref, *rest):
         seat = lax.axis_index("gy")
+        sems = rest[-1]
 
         def load(src):
-            copy = pltpu.make_async_copy(src.at[pl.ds((seat // 2) * rows, rows)], a_ref, sem)
-            copy.start()
-            copy.wait()
+            copies = [
+                pltpu.make_async_copy(
+                    src.at[pl.ds((seat // 2) * rows + c * part, part)], rest[c], sems.at[c]
+                )
+                for c in range(CHUNKS)
+            ]
+            for copy in copies:
+                copy.start()
+            for copy in copies:
+                copy.wait()
 
         @pl.when(seat % 2 == 0)
         def _():
@@ -77,11 +89,11 @@
 
     return call(
         kernel,
-        [((rows, width), F32)],
+        [((part, width), F32)] * CHUNKS,
         far=(operator, inverse),
-        scratch=[pltpu.SemaphoreType.DMA],
+        scratch=[pltpu.SemaphoreType.DMA((CHUNKS,))],
         flops=1 << 20,
-    )[0]
+    )
 
 
 def pack_blocks(operator, inverse, mobility, nodes):
@@ -154,6 +166,54 @@
         scratch=[pltpu.VMEM((4 * half, 4 * nodes), F32), pltpu.SemaphoreType.DMA((4,))],
         flops=1 << 20,
     )
+
+
+def choose(own, got, source, extra=None):
+    rows, width = own.shape
+    more = () if extra is None else (extra,)
+
+    def kernel(*refs):
+        out_ref = refs[-1]
+        gx = lax.axis_index("gx")
+        for target, ref in [(source, refs[0])] + list(zip(got, refs[1:])):
+            @pl.when(gx == target)
+            def _(ref=ref):
+                out_ref[pl.ds(0, rows), :] = ref[...]
+        if more:
+            out_ref[pl.ds(rows, extra.shape[0]), :] = refs[-2][...]
+
+    height = rows + (extra.shape[0] if more else 0)
+    return call(
+        kernel, [((height, width), F32)], values=(own, *got.values(), *more), flops=1 << 20
+    )[0]
+
+
+def gather_low(mids, smalls):
+    flat = [v for own, got, _ in mids for v in (own, *got.values())]
+    side = mids[0][0].shape[0]
+    lanes = smalls[0].shape[1]
+    start_small = len(mids) * 2 * side
+    height = start_small + len(smalls) * smalls[0].shape[0]
+
+    def kernel(*refs):
+        out_ref = refs[-1]
+        gx = lax.axis_index("gx")
+        at = 0
+        for j, (_, got, source) in enumerate(mids):
+            for target in [source] + list(got):
+                ref = refs[at]
+                at += 1
+
+                @pl.when(gx == target)
+                def _(ref=ref, j=j):
+                    for h in range(2):
+                        out_ref[pl.ds((2 * j + h) * side, side), :] = (
+                            ref[:, pl.ds(h * lanes, lanes)]
+                        )
+        for k in range(len(smalls)):
+            out_ref[pl.ds(start_small + k * lanes, lanes), :] = refs[at + k][...]
+
+    return call(kernel, [((height, lanes), F32)], values=(*flat, *smalls), flops=1 << 20)[0]
 
 
 def grade(buckets):
@@ -254,12 +314,19 @@
     return (length / count) * jnp.concatenate(sums + [zero, zero], axis=0)
 
 
-def solve_low(smalls, mids, sorted_small, sorted_mid, aux, slots, buckets, nodes):
+def solve_low(own, other, sorted_small, sorted_mid, aux, slots, buckets, nodes):
     small, mid, _ = grade(buckets)
     centres = slots.shape[1]
     half, quarter = nodes // 2, nodes // 4
 
-    def kernel(so_ref, st_ref, mo_ref, mt_ref, ss_ref, sm_ref, aux_ref, slot_ref, xs_ref, xm_ref, t_ref):
+    side = 4 * half
+    start_small = len(mid) * 2 * side
+
+    def mid_block(ref, j):
+        parts = [ref[pl.ds((2 * j + h) * side, side), :] for h in range(2)]
+        return jnp.concatenate(parts, axis=1)
+
+    def kernel(own_ref, other_ref, ss_ref, sm_ref, aux_ref, slot_ref, xs_ref, xm_ref, t_ref):
         gx = lax.axis_index("gx")
         first = lax.axis_index("gy") % 2 == 0
         systems, lengths, counts = [], [], []
@@ -267,11 +334,14 @@
             lanes = pl.ds(k * SLOT_CAP, SLOT_CAP)
             if k < len(small):
                 index = lax.rem(b - gx + buckets, buckets)
-                mine, theirs, ref, here, n = so_ref[index], st_ref[index], ss_ref, lanes, quarter
+                place = pl.ds(pl.multiple_of(start_small + index * nodes, nodes), nodes)
+                mine, theirs = own_ref[place, :], other_ref[place, :]
+                ref, here, n = ss_ref, lanes, quarter
             else:
                 j = k - len(small)
                 here = pl.ds(j * SLOT_CAP, SLOT_CAP)
-                mine, theirs, ref, n = mo_ref[j], mt_ref[j], sm_ref, half
+                mine, theirs = mid_block(own_ref, j), mid_block(other_ref, j)
+                ref, n = sm_ref, half
             systems.append(
                 (
                     split(jnp.where(first, mine, theirs)),
@@ -303,7 +373,7 @@
             ((4 * half, len(mid) * SLOT_CAP), F32),
             ((8, centres), F32),
         ],
-        values=(*smalls, *mids, sorted_small, sorted_mid, aux, slots),
+        values=(own, other, sorted_small, sorted_mid, aux, slots),
         flops=1 << 30,
     )
 
@@ -314,7 +384,8 @@
     width = LEVELS * nodes
     centres = slots.shape[1]
     shares = width // rows
-    flat = [p for pair in pieces for side in pair for p in side]
+    part = rows // CHUNKS
+    flat = [p for chunks in pieces for pair in chunks for side in pair for p in side]
 
     def kernel(*refs):
         piece_refs = refs[:len(flat)]
@@ -323,14 +394,14 @@
         chip, core = seat // 2, seat % 2
         total = tin_ref[...]
         for k in range(len(names)):
-            for side in range(2):
+            for i in range(CHUNKS * 2 * shares):
+                c, side, m = i // (2 * shares), (i // shares) % 2, i % shares
                 matrix = core if side == 0 else 1 - core
-                for m in range(shares):
-                    ref = piece_refs[(k * 2 + side) * shares + m]
-                    h, l = split(ref[pl.ds(0, rows), :])
-                    place = pl.ds(pl.multiple_of(jnp.bitwise_xor(chip, m) * rows, rows), rows)
-                    high[matrix, place, :] = h
-                    low[matrix, place, :] = l
+                h, l = split(piece_refs[k * CHUNKS * 2 * shares + i][pl.ds(0, part), :])
+                start = jnp.bitwise_xor(chip, m) * rows + c * part
+                place = pl.ds(pl.multiple_of(start, part), part)
+                high[matrix, place, :] = h
+                low[matrix, place, :] = l
             lanes = pl.ds(k * SLOT_CAP, SLOT_CAP)
             aux_lanes = pl.ds((n_low + k) * SLOT_CAP, SLOT_CAP)
             source = top_ref[pl.ds(0, width), lanes]
@@ -455,7 +526,6 @@
     seats = lax.axis_size("gy")
     chips = seats // 2
     rows = LEVELS * nodes // chips
-    gx = lax.axis_index("gx")
     centres = mobility.shape[1] * seats
     small, mid, top = grade(buckets)
 
@@ -463,24 +533,29 @@
         return lax.ppermute(value, "gy", [(i, i ^ m) for i in range(seats)])
 
     def spread(value, source):
-        mine = jnp.where(gx == source, value, 0.0)
+        got = {}
         for target in range(buckets):
             if target != source:
-                got = lax.ppermute(value, "gx", [(source, target)])
-                mine = mine + got
-        return mine
-
-    share = take_share(operator[0], inverse[0], rows)
-    shares = [spread(share, source) for source in top]
+                got[target] = lax.ppermute(value, "gx", [(source, target)])
+        return got
+
+    share_parts = take_share(operator[0], inverse[0], rows)
+    sent = [[spread(part, source) for part in share_parts] for source in top]
     block_mid, block_small, extra = pack_blocks(
         operator[0], inverse[0], mobility, nodes
     )
-    shares[0] = jnp.concatenate([shares[0], extra], axis=0)
-    mids = jnp.stack([spread(block_mid, source) for source in mid])
+    mids = [(block_mid, spread(block_mid, source), source) for source in mid]
+    shares = []
+    for k, source in enumerate(top):
+        for c, part in enumerate(share_parts):
+            shares.append(
+                choose(part, sent[k][c], source, extra if k == c == 0 else None)
+            )
     smalls = [block_small]
     for shift in range(1, buckets):
         smalls.append(lax.ppermute(block_small, "gx", [(s, (s - shift) % buckets) for s in small]))
-    smalls = jnp.stack(smalls)
+    own_low = gather_low(mids, smalls)
+    other_low = hop(own_low, 1)
 
     bucket_row = bucket.reshape(1, fibers)
     attach_row = attach.reshape(1, fibers)
@@ -490,23 +565,23 @@
     )
 
     pieces = []
-    for mine in shares:
+    for i, mine in enumerate(shares):
+        k, c = i // CHUNKS, i % CHUNKS
         own = [mine] + [hop(mine, 2 * m) for m in range(1, chips)]
         other = [hop(piece, 1) for piece in own]
-        pieces.append((own, other))
-
-    other_mids = hop(mids, 1)
-    other_smalls = hop(smalls, 1)
+        if c == 0:
+            pieces.append([])
+        pieces[k].append((own, other))
+
     x_small, x_mid, table_low = solve_low(
-        (smalls, other_smalls), (mids, other_mids), sorted_small, sorted_mid,
-        aux, slots, buckets, nodes,
+        own_low, other_low, sorted_small, sorted_mid, aux, slots, buckets, nodes
     )
     x_top, table = solve_top(pieces, sorted_top, aux, slots, table_low, buckets, nodes, rows)
 
     table = table + hop(table, 1)
     tables = [table] + [hop(table, 2 * m) for m in range(1, chips)]
     solved, mobility_all = unsort(
-        (x_small, x_mid, x_top), onehot, pieces[0], nodes, rows
+        (x_small, x_mid, x_top), onehot, pieces[0][0], nodes, rows // CHUNKS
     )
     return finish(tables, mobility_all, bucket_row, attach_row, offsets, solved, nodes)
 

time: 63.5 us -> 72 us (1.13)
  starting transfers between devices: 26.8 us -> 34.8 us
  local copies, waits for them, and re-layouts: 3.13 us -> 1.41 us
  Pallas kernels: 12.3 us -> 13.8 us
  waiting for transfers between devices: 20.4 us -> 21.3 us
    ppermute x13 -> x19, starting transfers between devices: 10.3 us -> 16.5 us  [hop(): return lax.ppermute(value, 'gy', [(i, i ^ m) for i in range(seats)])]
    ppermute x6 -> x9, waiting for transfers between devices: 6.39 us -> 10.6 us  [spread(): got[target] = lax.ppermute(value, 'gx', [(source, target)])]
    ppermute x13 -> x19, waiting for transfers between devices: 12.3 us -> 9.21 us  [hop(): return lax.ppermute(value, 'gy', [(i, i ^ m) for i in range(seats)])]
    ppermute x6 -> x9, starting transfers between devices: 5.28 us -> 8.03 us  [spread(): got[target] = lax.ppermute(value, 'gx', [(source, target)])]
    unnamed x16 -> x12, local copies, waits for them, and re-layouts: 3.13 us -> 1.41 us
    pallas_call x7 -> x10, Pallas kernels: 12.3 us -> 13.8 us  [call(): pl.pallas_call(kernel, out_shape=out_shape, in_specs=[FAR] * len(far) + [...]
    ppermute x3, starting transfers between devices: 11.3 us -> 10.3 us  [body(): lax.ppermute(block_small, 'gx', [(s, (s - shift) % buckets) for s in small])]
  transfers between devices with their start and end apart: 22 -> 31, of which waited for: 7 -> 8; matrix products, arithmetic and copies ran while one was open for 0% -> 0% of each run, Pallas kernels for 11% -> 10%
where the time goes in v1:
time: 72 us; the launch traced here: 71.6 us
  starting transfers between devices  34.8 us (48%)
  waiting for transfers between devices  21.3 us (30%)
  Pallas kernels  13.8 us (19%)
  local copies, waits for them, and re-layouts  1.41 us (2%)
    ppermute x19, starting transfers between devices, hop(): return lax.ppermute(value, 'gy', [(i, i ^ m) for i in range(seats)])  16.5 us
    pallas_call x10, Pallas kernels, call(): pl.pallas_call(kernel, out_shape=out_shape, in_specs=[FAR] * len(far) + [...  13.8 us
    ppermute x9, waiting for transfers between devices, spread(): got[target] = lax.ppermute(value, 'gx', [(source, target)])  10.6 us
    ppermute x3, starting transfers between devices, body(): lax.ppermute(block_small, 'gx', [(s, (s - shift) % buckets) for s in small])  10.3 us
    ppermute x19, waiting for transfers between devices, hop(): return lax.ppermute(value, 'gy', [(i, i ^ m) for i in range(seats)])  9.21 us
    ppermute x9, starting transfers between devices, spread(): got[target] = lax.ppermute(value, 'gx', [(source, target)])  8.03 us
    ppermute x3, waiting for transfers between devices, body(): lax.ppermute(block_small, 'gx', [(s, (s - shift) % buckets) for s in small])  1.53 us
  transfers between devices with their start and end apart: 31, of which 8 were waited for; matrix products, arithmetic and copies ran while one was open for 0% of the time, Pallas kernels for 10%

profile of v1, /device:TPU:0, one launch (start us, length us, event | category | flops | bytes accessed | tf_op | source)
XLA Modules:
  0.0 71.6 jit_solution(6423278132504930223)
XLA Ops:
  0.0 0.7 %copy-done.1 = f32[36,64]{1,0:T(8,128)S(1)} copy-done((f32[36,64]{1,0:T(8,128)S(1)}, f32[36,64]{1,0:T(8,128)}, u32[]{:S(2)}) %copy-start.1) | copy-done | bytes 9240
  0.7 1.3 %shard_map.83 = (f32[256,256]{1,0:T(8,128)S(1)}, f32[128,128]{1,0:T(8,128)S(1)}, f32[8,512]{1,0:T(8,128)S(1)}) custom-call(f32[512,512]{1,0:T(8,128)} %bitcast.10, f32[512,512]{1,0:T(8,128)} %bitcast.12, f32[36,64]{1,0:T(8,128)S(1)} %copy-done.1), custom_call_target="tpu_custom_call" | custom-call | flops 1048576 | bytes 1048576 | tf_op jit(solution)/shard_map/pallas_call | solution.py:50
  2.0 1.3 %collective-permute-start.20 = (f32[256,256]{1,0:T(8,128)S(1)}, f32[256,256]{1,0:T(8,128)S(1)}, u32[]{:S(2)}, u32[]{:S(2)}) collective-permute-start(f32[256,256]{1,0:T(8,128)S(1)} %get-tuple-element.29.refs_0_), channel_id=1, source_target_pairs={{16,0},{17,1},{18,2},{19,3},{20,4},{21,5},{22,6},{23,7}} | collective-permute-start | bytes 786440 | tf_op jit(solution)/shard_map/ppermute | solution.py:539
  3.4 0.7 collective-permute-start.21
  4.0 0.7 collective-permute-start.22
  4.7 7.0 %collective-permute-start.23 = (f32[128,128]{1,0:T(8,128)S(1)}, f32[128,128]{1,0:T(8,128)S(1)}, u32[]{:S(2)}, u32[]{:S(2)}) collective-permute-start(f32[128,128]{1,0:T(8,128)S(1)} %get-tuple-element.30.refs_4_), channel_id=1, source_target_pairs={{0,24},{8,0},{1,25},{9,1},{2,26},{10,2},{3,27},{11,3},{4,28},{12,4... | collective-permute-start | bytes 196616 | tf_op jit(solution)/shard_map/ppermute | solution.py:556
  11.7 1.9 %collective-permute-start.24 = (f32[128,128]{1,0:T(8,128)S(1)}, f32[128,128]{1,0:T(8,128)S(1)}, u32[]{:S(2)}, u32[]{:S(2)}) collective-permute-start(f32[128,128]{1,0:T(8,128)S(1)} %get-tuple-element.30.refs_4_), channel_id=1, source_target_pairs={{0,16},{8,24},{1,17},{9,25},{2,18},{10,26},{3,19},{11,27},{4,20},{... | collective-permute-start | bytes 196616 | tf_op jit(solution)/shard_map/ppermute | solution.py:556
  13.6 1.5 %collective-permute-done.23.refs_5_ = f32[128,128]{1,0:T(8,128)S(1)} collective-permute-done((f32[128,128]{1,0:T(8,128)S(1)}, f32[128,128]{1,0:T(8,128)S(1)}, u32[]{:S(2)}, u32[]{:S(2)}) %collective-permute-start.23) | collective-permute-done | bytes 65568 | tf_op jit(solution)/shard_map/ppermute | solution.py:556
  15.1 1.5 %collective-permute-start.25 = (f32[128,128]{1,0:T(8,128)S(1)}, f32[128,128]{1,0:T(8,128)S(1)}, u32[]{:S(2)}, u32[]{:S(2)}) collective-permute-start(f32[128,128]{1,0:T(8,128)S(1)} %get-tuple-element.30.refs_4_), channel_id=1, source_target_pairs={{0,8},{8,16},{1,9},{9,17},{2,10},{10,18},{3,11},{11,19},{4,12},{12... | collective-permute-start | bytes 196616 | tf_op jit(solution)/shard_map/ppermute | solution.py:556
  16.6 1.0 %shard_map.82 = (f32[64,512]{1,0:T(8,128)S(1)}, f32[64,512]{1,0:T(8,128)S(1)}) custom-call(f32[512,512]{1,0:T(8,128)} %bitcast.11, f32[512,512]{1,0:T(8,128)} %bitcast.13), custom_call_target="tpu_custom_call" | custom-call | flops 1048576 | bytes 1048576 | tf_op jit(solution)/shard_map/pallas_call | solution.py:50
  17.6 1.3 %collective-permute-start.10 = (f32[64,512]{1,0:T(8,128)S(1)}, f32[64,512]{1,0:T(8,128)S(1)}, u32[]{:S(2)}, u32[]{:S(2)}) collective-permute-start(f32[64,512]{1,0:T(8,128)S(1)} %get-tuple-element.25.refs_0_), channel_id=1, source_target_pairs={{24,0},{25,1},{26,2},{27,3},{28,4},{29,5},{30,6},{31,7}} | collective-permute-start | bytes 393224 | tf_op jit(solution)/shard_map/ppermute | solution.py:539
  18.9 0.7 collective-permute-start.11
  19.6 0.7 collective-permute-start.12
  20.3 0.0 copy-start.4
  20.3 0.1 shard_map.87.own_ref
  20.4 0.1 collective-permute-start.26
  20.5 1.4 %collective-permute-start = (f32[64,512]{1,0:T(8,128)S(1)}, f32[64,512]{1,0:T(8,128)S(1)}, u32[]{:S(2)}, u32[]{:S(2)}) collective-permute-start(f32[64,512]{1,0:T(8,128)S(1)} %get-tuple-element.23.refs_0_), channel_id=1, source_target_pairs={{24,0},{25,1},{26,2},{27,3},{28,4},{29,5},{30,6},{31,7}} | collective-permute-start | bytes 393224 | tf_op jit(solution)/shard_map/ppermute | solution.py:539
  21.9 5.8 %collective-permute-done.10.refs_1_ = f32[64,512]{1,0:T(8,128)S(1)} collective-permute-done((f32[64,512]{1,0:T(8,128)S(1)}, f32[64,512]{1,0:T(8,128)S(1)}, u32[]{:S(2)}, u32[]{:S(2)}) %collective-permute-start.10) | collective-permute-done | bytes 131104 | tf_op jit(solution)/shard_map/ppermute | solution.py:539
  27.7 0.7 collective-permute-start.1
  28.3 0.7 collective-permute-start.2
  29.1 2.2 %collective-permute-start.13 = (f32[64,512]{1,0:T(8,128)S(1)}, f32[64,512]{1,0:T(8,128)S(1)}, u32[]{:S(2)}, u32[]{:S(2)}) collective-permute-start(f32[64,512]{1,0:T(8,128)S(1)} %shard_map.85.refs_8_), channel_id=1, source_target_pairs={{0,2},{1,3},{2,0},{3,1},{4,6},{5,7},{6,4},{7,5},{8,10},{9,11},{10,... | collective-permute-start | bytes 393224 | tf_op jit(solution)/shard_map/ppermute | solution.py:533
  31.3 4.8 %collective-permute-done.refs_1_ = f32[64,512]{1,0:T(8,128)S(1)} collective-permute-done((f32[64,512]{1,0:T(8,128)S(1)}, f32[64,512]{1,0:T(8,128)S(1)}, u32[]{:S(2)}, u32[]{:S(2)}) %collective-permute-start) | collective-permute-done | bytes 131104 | tf_op jit(solution)/shard_map/ppermute | solution.py:539
  36.1 2.2 %collective-permute-start.14 = (f32[64,512]{1,0:T(8,128)S(1)}, f32[64,512]{1,0:T(8,128)S(1)}, u32[]{:S(2)}, u32[]{:S(2)}) collective-permute-start(f32[64,512]{1,0:T(8,128)S(1)} %shard_map.85.refs_8_), channel_id=1, source_target_pairs={{0,4},{1,5},{2,6},{3,7},{4,0},{5,1},{6,2},{7,3},{8,12},{9,13},{10,... | collective-permute-start | bytes 393224 | tf_op jit(solution)/shard_map/ppermute | solution.py:533
  38.3 1.4 %collective-permute-start.15 = (f32[64,512]{1,0:T(8,128)S(1)}, f32[64,512]{1,0:T(8,128)S(1)}, u32[]{:S(2)}, u32[]{:S(2)}) collective-permute-start(f32[64,512]{1,0:T(8,128)S(1)} %shard_map.85.refs_8_), channel_id=1, source_target_pairs={{0,6},{1,7},{2,4},{3,5},{4,2},{5,3},{6,0},{7,1},{8,14},{9,15},{10,... | collective-permute-start | bytes 393224 | tf_op jit(solution)/shard_map/ppermute | solution.py:533
  39.8 0.2 collective-permute-start.3
  40.0 2.2 %collective-permute-done.14.refs_10_ = f32[64,512]{1,0:T(8,128)S(1)} collective-permute-done((f32[64,512]{1,0:T(8,128)S(1)}, f32[64,512]{1,0:T(8,128)S(1)}, u32[]{:S(2)}, u32[]{:S(2)}) %collective-permute-start.14) | collective-permute-done | bytes 131104 | tf_op jit(solution)/shard_map/ppermute | solution.py:533
  42.2 2.4 %collective-permute-start.4 = (f32[72,512]{1,0:T(8,128)S(1)}, f32[72,512]{1,0:T(8,128)S(1)}, u32[]{:S(2)}, u32[]{:S(2)}) collective-permute-start(f32[72,512]{1,0:T(8,128)S(1)} %shard_map.84.refs_0_.refs_4_), channel_id=1, source_target_pairs={{0,4},{1,5},{2,6},{3,7},{4,0},{5,1},{6,2},{7,3},{8,12},{9,13},{10,... | collective-permute-start | bytes 442376 | tf_op jit(solution)/shard_map/ppermute | solution.py:533
  44.6 2.3 %collective-permute-start.5 = (f32[72,512]{1,0:T(8,128)S(1)}, f32[72,512]{1,0:T(8,128)S(1)}, u32[]{:S(2)}, u32[]{:S(2)}) collective-permute-start(f32[72,512]{1,0:T(8,128)S(1)} %shard_map.84.refs_0_.refs_4_), channel_id=1, source_target_pairs={{0,6},{1,7},{2,4},{3,5},{4,2},{5,3},{6,0},{7,1},{8,14},{9,15},{10,... | collective-permute-start | bytes 442376 | tf_op jit(solution)/shard_map/ppermute | solution.py:533
  47.0 0.5 collective-permute-start.17
  47.5 3.4 %collective-permute-done.4.refs_2_.refs_6_ = f32[72,512]{1,0:T(8,128)S(1)} collective-permute-done((f32[72,512]{1,0:T(8,128)S(1)}, f32[72,512]{1,0:T(8,128)S(1)}, u32[]{:S(2)}, u32[]{:S(2)}) %collective-permute-start.4) | collective-permute-done | bytes 147488 | tf_op jit(solution)/shard_map/ppermute | solution.py:533
  50.9 0.5 collective-permute-start.19
  51.4 0.1 collective-permute-start.7
  51.5 0.4 collective-permute-start.8
  52.0 0.1 collective-permute-start.9
  52.1 0.7 copy-done.2
  52.7 3.1 %shard_map.86 = (bf16[512,512]{1,0:T(8,128)(2,1)S(1)}, bf16[512,512]{1,0:T(8,128)(2,1)S(1)}, f32[224,256]{1,0:T(8,128)S(1)}, f32[448,128]{1,0:T(8,128)S(1)}, f32...) custom-call(s32[1,512]{1,0:T(1,128)S(1)} %bitcast.5, s32[1,512]{1,0:T(1,128)S(1)} %bitcast.7, f32[1,512]{1,0:T(1,128)S(1)} %bitcast.9, ...), custom_call_target="tpu_custom_call" | custom-call | flops 1073741824 | bytes 1048576 | tf_op jit(solution)/shard_map/pallas_call | solution.py:50
  55.8 2.1 %shard_map.88 = (f32[128,256]{1,0:T(8,128)S(1)}, f32[256,128]{1,0:T(8,128)S(1)}, f32[8,512]{1,0:T(8,128)S(1)}) custom-call(f32[1024,128]{1,0:T(8,128)S(1)} %shard_map.87.own_ref, f32[1024,128]{1,0:T(8,128)S(1)} %collective-permute-done.26.other_ref, f32[224,256]{1,0:T(8,128)S(1)} %get-tuple-element.31.ss_ref, f32[448,128]{1,0:T(8,128)S(1)} %get-tuple-element.32.sm_ref, ...), custom_call_target="tpu_custom_call" | custom-call | flops 1073741824 | bytes 1048576 | tf_op jit(solution)/shard_map/pallas_call | solution.py:50
  57.9 0.0 collective-permute-done.7.refs_5_.refs_9_
  58.0 3.7 %shard_map.89 = (f32[512,128]{1,0:T(8,128)S(1)}, f32[8,512]{1,0:T(8,128)S(1)}) custom-call(f32[72,512]{1,0:T(8,128)S(1)} %shard_map.84.refs_0_.refs_4_, f32[72,512]{1,0:T(8,128)S(1)} %collective-permute-done.3.refs_1_.refs_5_, f32[72,512]{1,0:T(8,128)S(1)} %collective-permute-done.4.refs_2_.refs_6_, f32[72,512]{1,0:T(8,128)S(1)} %collective-permute-done.5.refs_3_.refs_7_, ...), custom_call_target="tpu_custom_call" | custom-call | flops 2147483648 | bytes 1048576 | tf_op jit(solution)/shard_map/pallas_call | solution.py:50
  61.7 0.5 collective-permute-start.27
  62.2 0.8 %collective-permute-done.27 = f32[8,512]{1,0:T(8,128)S(1)} collective-permute-done((f32[8,512]{1,0:T(8,128)S(1)}, f32[8,512]{1,0:T(8,128)S(1)}, u32[]{:S(2)}, u32[]{:S(2)}) %collective-permute-start.27) | collective-permute-done | bytes 16416 | tf_op jit(solution)/shard_map/ppermute | solution.py:533
  63.0 1.8 %collective-permute-start.28 = (f32[8,512]{1,0:T(8,128)S(1)}, f32[8,512]{1,0:T(8,128)S(1)}, u32[]{:S(2)}, u32[]{:S(2)}) collective-permute-start(f32[8,512]{1,0:T(8,128)S(1)} %add.3.refs_0_), channel_id=1, source_target_pairs={{0,2},{1,3},{2,0},{3,1},{4,6},{5,7},{6,4},{7,5},{8,10},{9,11},{10,... | collective-permute-start | bytes 49160 | tf_op jit(solution)/shard_map/ppermute | solution.py:533
  64.8 0.7 collective-permute-start.29
  65.5 1.0 %collective-permute-start.30 = (f32[8,512]{1,0:T(8,128)S(1)}, f32[8,512]{1,0:T(8,128)S(1)}, u32[]{:S(2)}, u32[]{:S(2)}) collective-permute-start(f32[8,512]{1,0:T(8,128)S(1)} %add.3.refs_0_), channel_id=1, source_target_pairs={{0,6},{1,7},{2,4},{3,5},{4,2},{5,3},{6,0},{7,1},{8,14},{9,15},{10,... | collective-permute-start | bytes 49160 | tf_op jit(solution)/shard_map/ppermute | solution.py:533
  66.5 0.9 %shard_map.90 = (f32[4,128,512]{2,1,0:T(8,128)S(1)}, f32[40,512]{1,0:T(8,128)S(1)}) custom-call(f32[128,256]{1,0:T(8,128)S(1)} %get-tuple-element.35.refs_0_, f32[256,128]{1,0:T(8,128)S(1)} %get-tuple-element.36.refs_1_, f32[512,128]{1,0:T(8,128)S(1)} %get-tuple-element.37.refs_2_, bf16[512,512]{1,0:T(8,128)(2,1)S(1)} %get-tuple-element.38.refs_3_, ...), custom_call_target="tpu_custom_call" | custom-call | flops 268435456 | bytes 1048576 | tf_op jit(solution)/shard_map/pallas_call | solution.py:50
  67.4 1.1 %collective-permute-done.29.refs_2_ = f32[8,512]{1,0:T(8,128)S(1)} collective-permute-done((f32[8,512]{1,0:T(8,128)S(1)}, f32[8,512]{1,0:T(8,128)S(1)}, u32[]{:S(2)}, u32[]{:S(2)}) %collective-permute-start.29) | collective-permute-done | bytes 16416 | tf_op jit(solution)/shard_map/ppermute | solution.py:533
  68.5 1.6 %collective-permute-done.30.refs_3_ = f32[8,512]{1,0:T(8,128)S(1)} collective-permute-done((f32[8,512]{1,0:T(8,128)S(1)}, f32[8,512]{1,0:T(8,128)S(1)}, u32[]{:S(2)}, u32[]{:S(2)}) %collective-permute-start.30) | collective-permute-done | bytes 16416 | tf_op jit(solution)/shard_map/ppermute | solution.py:533
  70.1 1.5 %shard_map.91 = f32[4,128,512]{2,1,0:T(8,128)} custom-call(f32[8,512]{1,0:T(8,128)S(1)} %add.3.refs_0_, f32[8,512]{1,0:T(8,128)S(1)} %collective-permute-done.28.refs_1_, f32[8,512]{1,0:T(8,128)S(1)} %collective-permute-done.29.refs_2_, f32[8,512]{1,0:T(8,128)S(1)} %collective-permute-done.30.refs_3_, f32[40,512]{1,0:T(8,128)S(1)} %get-tuple-element.39.refs_4_, ...), custom_call_target="tpu_custom_call" | custom-call | flops 16777216 | bytes 1048576 | tf_op jit(solution)/shard_map/pallas_call | solution.py:50
  (37 shorter events, 0.2 us)
Async XLA Ops:
  0.0 0.7 %copy-start.1 = (f32[36,64]{1,0:T(8,128)S(1)}, f32[36,64]{1,0:T(8,128)}, u32[]{:S(2)}) copy-start(f32[36,64]{1,0:T(8,128)} %mob_ref.1) | copy-start | bytes 27652
  2.0 17.5 %collective-permute-start.20 = (f32[256,256]{1,0:T(8,128)S(1)}, f32[256,256]{1,0:T(8,128)S(1)}, u32[]{:S(2)}, u32[]{:S(2)}) collective-permute-start(f32[256,256]{1,0:T(8,128)S(1)} %get-tuple-element.29.refs_0_), channel_id=1, source_target_pairs={{16,0},{17,1},{18,2},{19,3},{20,4},{21,5},{22,6},{23,7}} | collective-permute-start | bytes 786440 | tf_op jit(solution)/shard_map/ppermute | solution.py:539
  3.4 16.9 %collective-permute-start.21 = (f32[256,256]{1,0:T(8,128)S(1)}, f32[256,256]{1,0:T(8,128)S(1)}, u32[]{:S(2)}, u32[]{:S(2)}) collective-permute-start(f32[256,256]{1,0:T(8,128)S(1)} %get-tuple-element.29.refs_0_), channel_id=1, source_target_pairs={{16,8},{17,9},{18,10},{19,11},{20,12},{21,13},{22,14},{23,15}} | collective-permute-start | bytes 786440 | tf_op jit(solution)/shard_map/ppermute | solution.py:539
  4.0 16.3 %collective-permute-start.22 = (f32[256,256]{1,0:T(8,128)S(1)}, f32[256,256]{1,0:T(8,128)S(1)}, u32[]{:S(2)}, u32[]{:S(2)}) collective-permute-start(f32[256,256]{1,0:T(8,128)S(1)} %get-tuple-element.29.refs_0_), channel_id=1, source_target_pairs={{16,24},{17,25},{18,26},{19,27},{20,28},{21,29},{22,30},{23,31}} | collective-permute-start | bytes 786440 | tf_op jit(solution)/shard_map/ppermute | solution.py:539
  4.7 10.4 %collective-permute-start.23 = (f32[128,128]{1,0:T(8,128)S(1)}, f32[128,128]{1,0:T(8,128)S(1)}, u32[]{:S(2)}, u32[]{:S(2)}) collective-permute-start(f32[128,128]{1,0:T(8,128)S(1)} %get-tuple-element.30.refs_4_), channel_id=1, source_target_pairs={{0,24},{8,0},{1,25},{9,1},{2,26},{10,2},{3,27},{11,3},{4,28},{12,4... | collective-permute-start | bytes 196616 | tf_op jit(solution)/shard_map/ppermute | solution.py:556
  11.7 5.9 %collective-permute-start.24 = (f32[128,128]{1,0:T(8,128)S(1)}, f32[128,128]{1,0:T(8,128)S(1)}, u32[]{:S(2)}, u32[]{:S(2)}) collective-permute-start(f32[128,128]{1,0:T(8,128)S(1)} %get-tuple-element.30.refs_4_), channel_id=1, source_target_pairs={{0,16},{8,24},{1,17},{9,25},{2,18},{10,26},{3,19},{11,27},{4,20},{... | collective-permute-start | bytes 196616 | tf_op jit(solution)/shard_map/ppermute | solution.py:556
  15.1 3.8 %collective-permute-start.25 = (f32[128,128]{1,0:T(8,128)S(1)}, f32[128,128]{1,0:T(8,128)S(1)}, u32[]{:S(2)}, u32[]{:S(2)}) collective-permute-start(f32[128,128]{1,0:T(8,128)S(1)} %get-tuple-element.30.refs_4_), channel_id=1, source_target_pairs={{0,8},{8,16},{1,9},{9,17},{2,10},{10,18},{3,11},{11,19},{4,12},{12... | collective-permute-start | bytes 196616 | tf_op jit(solution)/shard_map/ppermute | solution.py:556
  17.6 10.1 %collective-permute-start.10 = (f32[64,512]{1,0:T(8,128)S(1)}, f32[64,512]{1,0:T(8,128)S(1)}, u32[]{:S(2)}, u32[]{:S(2)}) collective-permute-start(f32[64,512]{1,0:T(8,128)S(1)} %get-tuple-element.25.refs_0_), channel_id=1, source_target_pairs={{24,0},{25,1},{26,2},{27,3},{28,4},{29,5},{30,6},{31,7}} | collective-permute-start | bytes 393224 | tf_op jit(solution)/shard_map/ppermute | solution.py:539
  18.9 9.4 %collective-permute-start.11 = (f32[64,512]{1,0:T(8,128)S(1)}, f32[64,512]{1,0:T(8,128)S(1)}, u32[]{:S(2)}, u32[]{:S(2)}) collective-permute-start(f32[64,512]{1,0:T(8,128)S(1)} %get-tuple-element.25.refs_0_), channel_id=1, source_target_pairs={{24,8},{25,9},{26,10},{27,11},{28,12},{29,13},{30,14},{31,15}} | collective-permute-start | bytes 393224 | tf_op jit(solution)/shard_map/ppermute | solution.py:539
  19.6 9.4 %collective-permute-start.12 = (f32[64,512]{1,0:T(8,128)S(1)}, f32[64,512]{1,0:T(8,128)S(1)}, u32[]{:S(2)}, u32[]{:S(2)}) collective-permute-start(f32[64,512]{1,0:T(8,128)S(1)} %get-tuple-element.25.refs_0_), channel_id=1, source_target_pairs={{24,16},{25,17},{26,18},{27,19},{28,20},{29,21},{30,22},{31,23}} | collective-permute-start | bytes 393224 | tf_op jit(solution)/shard_map/ppermute | solution.py:539
  20.3 31.7 %copy-start.4 = (f32[4,128,512]{2,1,0:T(8,128)S(1)}, f32[4,128,512]{2,1,0:T(8,128)}, u32[]{:S(2)}) copy-start(f32[4,128,512]{2,1,0:T(8,128)} %rhs_ref.1) | copy-start | bytes 3145732
  20.4 31.7 %copy-start = (f32[3,128,512]{2,1,0:T(8,128)S(1)}, f32[3,128,512]{2,1,0:T(8,128)}, u32[]{:S(2)}) copy-start(f32[3,128,512]{2,1,0:T(8,128)} %refs_7_.1) | copy-start | bytes 2359300
  20.4 31.6 %collective-permute-start.26 = (f32[1024,128]{1,0:T(8,128)S(1)}, f32[1024,128]{1,0:T(8,128)S(1)}, u32[]{:S(2)}, u32[]{:S(2)}) collective-permute-start(f32[1024,128]{1,0:T(8,128)S(1)} %shard_map.87.own_ref), channel_id=1, source_target_pairs={{0,1},{1,0},{2,3},{3,2},{4,5},{5,4},{6,7},{7,6},{8,9},{9,8},{10,11... | collective-permute-start | bytes 1572872 | tf_op jit(solution)/shard_map/ppermute | solution.py:533
  20.5 15.6 %collective-permute-start = (f32[64,512]{1,0:T(8,128)S(1)}, f32[64,512]{1,0:T(8,128)S(1)}, u32[]{:S(2)}, u32[]{:S(2)}) collective-permute-start(f32[64,512]{1,0:T(8,128)S(1)} %get-tuple-element.23.refs_0_), channel_id=1, source_target_pairs={{24,0},{25,1},{26,2},{27,3},{28,4},{29,5},{30,6},{31,7}} | collective-permute-start | bytes 393224 | tf_op jit(solution)/shard_map/ppermute | solution.py:539
  27.7 10.6 %collective-permute-start.1 = (f32[64,512]{1,0:T(8,128)S(1)}, f32[64,512]{1,0:T(8,128)S(1)}, u32[]{:S(2)}, u32[]{:S(2)}) collective-permute-start(f32[64,512]{1,0:T(8,128)S(1)} %get-tuple-element.23.refs_0_), channel_id=1, source_target_pairs={{24,8},{25,9},{26,10},{27,11},{28,12},{29,13},{30,14},{31,15}} | collective-permute-start | bytes 393224 | tf_op jit(solution)/shard_map/ppermute | solution.py:539
  28.3 11.4 %collective-permute-start.2 = (f32[64,512]{1,0:T(8,128)S(1)}, f32[64,512]{1,0:T(8,128)S(1)}, u32[]{:S(2)}, u32[]{:S(2)}) collective-permute-start(f32[64,512]{1,0:T(8,128)S(1)} %get-tuple-element.23.refs_0_), channel_id=1, source_target_pairs={{24,16},{25,17},{26,18},{27,19},{28,20},{29,21},{30,22},{31,23}} | collective-permute-start | bytes 393224 | tf_op jit(solution)/shard_map/ppermute | solution.py:539
  29.1 10.7 %collective-permute-start.13 = (f32[64,512]{1,0:T(8,128)S(1)}, f32[64,512]{1,0:T(8,128)S(1)}, u32[]{:S(2)}, u32[]{:S(2)}) collective-permute-start(f32[64,512]{1,0:T(8,128)S(1)} %shard_map.85.refs_8_), channel_id=1, source_target_pairs={{0,2},{1,3},{2,0},{3,1},{4,6},{5,7},{6,4},{7,5},{8,10},{9,11},{10,... | collective-permute-start | bytes 393224 | tf_op jit(solution)/shard_map/ppermute | solution.py:533
  36.1 6.1 %collective-permute-start.14 = (f32[64,512]{1,0:T(8,128)S(1)}, f32[64,512]{1,0:T(8,128)S(1)}, u32[]{:S(2)}, u32[]{:S(2)}) collective-permute-start(f32[64,512]{1,0:T(8,128)S(1)} %shard_map.85.refs_8_), channel_id=1, source_target_pairs={{0,4},{1,5},{2,6},{3,7},{4,0},{5,1},{6,2},{7,3},{8,12},{9,13},{10,... | collective-permute-start | bytes 393224 | tf_op jit(solution)/shard_map/ppermute | solution.py:533
  38.3 6.4 %collective-permute-start.15 = (f32[64,512]{1,0:T(8,128)S(1)}, f32[64,512]{1,0:T(8,128)S(1)}, u32[]{:S(2)}, u32[]{:S(2)}) collective-permute-start(f32[64,512]{1,0:T(8,128)S(1)} %shard_map.85.refs_8_), channel_id=1, source_target_pairs={{0,6},{1,7},{2,4},{3,5},{4,2},{5,3},{6,0},{7,1},{8,14},{9,15},{10,... | collective-permute-start | bytes 393224 | tf_op jit(solution)/shard_map/ppermute | solution.py:533
  39.7 7.3 %collective-permute-start.16 = (f32[64,512]{1,0:T(8,128)S(1)}, f32[64,512]{1,0:T(8,128)S(1)}, u32[]{:S(2)}, u32[]{:S(2)}) collective-permute-start(f32[64,512]{1,0:T(8,128)S(1)} %shard_map.85.refs_8_), channel_id=1, source_target_pairs={{0,1},{1,0},{2,3},{3,2},{4,5},{5,4},{6,7},{7,6},{8,9},{9,8},{10,11... | collective-permute-start | bytes 393224 | tf_op jit(solution)/shard_map/ppermute | solution.py:533
  39.7 12.3 %copy-start.3 = (s32[512]{0:T(512)S(1)}, s32[512]{0:T(512)}, u32[]{:S(2)}) copy-start(s32[512]{0:T(512)} %param.12) | copy-start | bytes 6148
  39.7 12.3 %copy-start.5 = (f32[512]{0:T(512)S(1)}, f32[512]{0:T(512)}, u32[]{:S(2)}) copy-start(f32[512]{0:T(512)} %param.10) | copy-start | bytes 6148
  39.8 7.2 %collective-permute-start.3 = (f32[72,512]{1,0:T(8,128)S(1)}, f32[72,512]{1,0:T(8,128)S(1)}, u32[]{:S(2)}, u32[]{:S(2)}) collective-permute-start(f32[72,512]{1,0:T(8,128)S(1)} %shard_map.84.refs_0_.refs_4_), channel_id=1, source_target_pairs={{0,2},{1,3},{2,0},{3,1},{4,6},{5,7},{6,4},{7,5},{8,10},{9,11},{10,... | collective-permute-start | bytes 442376 | tf_op jit(solution)/shard_map/ppermute | solution.py:533
  42.2 8.7 %collective-permute-start.4 = (f32[72,512]{1,0:T(8,128)S(1)}, f32[72,512]{1,0:T(8,128)S(1)}, u32[]{:S(2)}, u32[]{:S(2)}) collective-permute-start(f32[72,512]{1,0:T(8,128)S(1)} %shard_map.84.refs_0_.refs_4_), channel_id=1, source_target_pairs={{0,4},{1,5},{2,6},{3,7},{4,0},{5,1},{6,2},{7,3},{8,12},{9,13},{10,... | collective-permute-start | bytes 442376 | tf_op jit(solution)/shard_map/ppermute | solution.py:533
  44.6 6.3 %collective-permute-start.5 = (f32[72,512]{1,0:T(8,128)S(1)}, f32[72,512]{1,0:T(8,128)S(1)}, u32[]{:S(2)}, u32[]{:S(2)}) collective-permute-start(f32[72,512]{1,0:T(8,128)S(1)} %shard_map.84.refs_0_.refs_4_), channel_id=1, source_target_pairs={{0,6},{1,7},{2,4},{3,5},{4,2},{5,3},{6,0},{7,1},{8,14},{9,15},{10,... | collective-permute-start | bytes 442376 | tf_op jit(solution)/shard_map/ppermute | solution.py:533
  47.0 4.5 %collective-permute-start.6 = (f32[72,512]{1,0:T(8,128)S(1)}, f32[72,512]{1,0:T(8,128)S(1)}, u32[]{:S(2)}, u32[]{:S(2)}) collective-permute-start(f32[72,512]{1,0:T(8,128)S(1)} %shard_map.84.refs_0_.refs_4_), channel_id=1, source_target_pairs={{0,1},{1,0},{2,3},{3,2},{4,5},{5,4},{6,7},{7,6},{8,9},{9,8},{10,11... | collective-permute-start | bytes 442376 | tf_op jit(solution)/shard_map/ppermute | solution.py:533
  47.0 4.5 %collective-permute-start.17 = (f32[64,512]{1,0:T(8,128)S(1)}, f32[64,512]{1,0:T(8,128)S(1)}, u32[]{:S(2)}, u32[]{:S(2)}) collective-permute-start(f32[64,512]{1,0:T(8,128)S(1)} %collective-permute-done.13.refs_9_), channel_id=1, source_target_pairs={{0,1},{1,0},{2,3},{3,2},{4,5},{5,4},{6,7},{7,6},{8,9},{9,8},{10,11... | collective-permute-start | bytes 393224 | tf_op jit(solution)/shard_map/ppermute | solution.py:533
  50.9 7.0 %collective-permute-start.18 = (f32[64,512]{1,0:T(8,128)S(1)}, f32[64,512]{1,0:T(8,128)S(1)}, u32[]{:S(2)}, u32[]{:S(2)}) collective-permute-start(f32[64,512]{1,0:T(8,128)S(1)} %collective-permute-done.14.refs_10_), channel_id=1, source_target_pairs={{0,1},{1,0},{2,3},{3,2},{4,5},{5,4},{6,7},{7,6},{8,9},{9,8},{10,11... | collective-permute-start | bytes 393224 | tf_op jit(solution)/shard_map/ppermute | solution.py:533
  50.9 7.0 %collective-permute-start.19 = (f32[64,512]{1,0:T(8,128)S(1)}, f32[64,512]{1,0:T(8,128)S(1)}, u32[]{:S(2)}, u32[]{:S(2)}) collective-permute-start(f32[64,512]{1,0:T(8,128)S(1)} %collective-permute-done.15.refs_11_), channel_id=1, source_target_pairs={{0,1},{1,0},{2,3},{3,2},{4,5},{5,4},{6,7},{7,6},{8,9},{9,8},{10,11... | collective-permute-start | bytes 393224 | tf_op jit(solution)/shard_map/ppermute | solution.py:533
  51.4 6.5 %collective-permute-start.7 = (f32[72,512]{1,0:T(8,128)S(1)}, f32[72,512]{1,0:T(8,128)S(1)}, u32[]{:S(2)}, u32[]{:S(2)}) collective-permute-start(f32[72,512]{1,0:T(8,128)S(1)} %collective-permute-done.3.refs_1_.refs_5_), channel_id=1, source_target_pairs={{0,1},{1,0},{2,3},{3,2},{4,5},{5,4},{6,7},{7,6},{8,9},{9,8},{10,11... | collective-permute-start | bytes 442376 | tf_op jit(solution)/shard_map/ppermute | solution.py:533
  51.5 6.4 %collective-permute-start.8 = (f32[72,512]{1,0:T(8,128)S(1)}, f32[72,512]{1,0:T(8,128)S(1)}, u32[]{:S(2)}, u32[]{:S(2)}) collective-permute-start(f32[72,512]{1,0:T(8,128)S(1)} %collective-permute-done.4.refs_2_.refs_6_), channel_id=1, source_target_pairs={{0,1},{1,0},{2,3},{3,2},{4,5},{5,4},{6,7},{7,6},{8,9},{9,8},{10,11... | collective-permute-start | bytes 442376 | tf_op jit(solution)/shard_map/ppermute | solution.py:533
  52.0 6.0 %collective-permute-start.9 = (f32[72,512]{1,0:T(8,128)S(1)}, f32[72,512]{1,0:T(8,128)S(1)}, u32[]{:S(2)}, u32[]{:S(2)}) collective-permute-start(f32[72,512]{1,0:T(8,128)S(1)} %collective-permute-done.5.refs_3_.refs_7_), channel_id=1, source_target_pairs={{0,1},{1,0},{2,3},{3,2},{4,5},{5,4},{6,7},{7,6},{8,9},{9,8},{10,11... | collective-permute-start | bytes 442376 | tf_op jit(solution)/shard_map/ppermute | solution.py:533
  52.0 0.7 copy-start.2
  61.7 1.3 %collective-permute-start.27 = (f32[8,512]{1,0:T(8,128)S(1)}, f32[8,512]{1,0:T(8,128)S(1)}, u32[]{:S(2)}, u32[]{:S(2)}) collective-permute-start(f32[8,512]{1,0:T(8,128)S(1)} %get-tuple-element.34), channel_id=1, source_target_pairs={{0,1},{1,0},{2,3},{3,2},{4,5},{5,4},{6,7},{7,6},{8,9},{9,8},{10,11... | collective-permute-start | bytes 49160 | tf_op jit(solution)/shard_map/ppermute | solution.py:533
  63.0 4.4 %collective-permute-start.28 = (f32[8,512]{1,0:T(8,128)S(1)}, f32[8,512]{1,0:T(8,128)S(1)}, u32[]{:S(2)}, u32[]{:S(2)}) collective-permute-start(f32[8,512]{1,0:T(8,128)S(1)} %add.3.refs_0_), channel_id=1, source_target_pairs={{0,2},{1,3},{2,0},{3,1},{4,6},{5,7},{6,4},{7,5},{8,10},{9,11},{10,... | collective-permute-start | bytes 49160 | tf_op jit(solution)/shard_map/ppermute | solution.py:533
  64.8 3.7 %collective-permute-start.29 = (f32[8,512]{1,0:T(8,128)S(1)}, f32[8,512]{1,0:T(8,128)S(1)}, u32[]{:S(2)}, u32[]{:S(2)}) collective-permute-start(f32[8,512]{1,0:T(8,128)S(1)} %add.3.refs_0_), channel_id=1, source_target_pairs={{0,4},{1,5},{2,6},{3,7},{4,0},{5,1},{6,2},{7,3},{8,12},{9,13},{10,... | collective-permute-start | bytes 49160 | tf_op jit(solution)/shard_map/ppermute | solution.py:533
  65.5 4.6 %collective-permute-start.30 = (f32[8,512]{1,0:T(8,128)S(1)}, f32[8,512]{1,0:T(8,128)S(1)}, u32[]{:S(2)}, u32[]{:S(2)}) collective-permute-start(f32[8,512]{1,0:T(8,128)S(1)} %add.3.refs_0_), channel_id=1, source_target_pairs={{0,6},{1,7},{2,4},{3,5},{4,2},{5,3},{6,0},{7,1},{8,14},{9,15},{10,... | collective-permute-start | bytes 49160 | tf_op jit(solution)/shard_map/ppermute | solution.py:533
